TPU v7x, 32 devices: a whole 2x2x4 slice. The times are simulated.
32 devices in a mesh: tile: 8 (over z, x), conv: 4 (over y, core).
Axes of the slice: x: 2, y: 2, z: 4, core: 2. Of those that a mesh axis runs over, the one named last changes fastest.
Arguments:
- field: float32 [256, 24576], P(None, ('tile', 'conv')), may hold values from -6 to 6
- interp: bfloat16 [32768, 384], P(('tile', 'conv')), may hold values from -0.1875 to 0.1875
- conv_blocks: bfloat16 [64, 3, 256, 256], P(('tile', 'conv')), may hold values from -0.21875 to 0.21875
- band_shift: int32 [64, 3], P(('tile', 'conv')), may hold values from 0 to 1
- owner: int32 [12288, 1], P(('tile', 'conv')), may hold values from 0 to 3; in each aligned block of 384 rows (0 to 383, 384 to 767, ...) at most 128 rows name the same one
- edge_index: int32 [64, 128], P(('tile', 'conv')), may hold values from 0 to 767, as said below
Outputs:
- correlated: float32 [256, 24576], P(None, ('tile', 'conv'))
Inputs may be any that keep to these rules, and one draw needn't show every extreme that they name: `edge_index`: row 2b lists the first 128 columns of domain b in some order, row 2b + 1 its last 128 columns in some order. Among the 384 points of one domain no owner is named more than 128 times, and in some domains one owner is named exactly 128 times.
All inputs are finite; a program needn't handle non-finite values.
Results may differ from a plain program's by a relative error of at most 0.0049.
Values may be sent and summed in bfloat16 or wider, within the bound.
A program may use at most 64 MiB of HBM per device.

v0:
```python
import functools

import jax
import jax.numpy as jnp
from jax import lax
from jax.experimental import pallas as pl
from jax.experimental.pallas import tpu as pltpu
from jax.sharding import PartitionSpec as P

MESH = pl.DeviceIdType.MESH
CHUNKS = 2


def mm(left, right):
    return lax.dot_general(left, right, (((1,), (0,)), ((), ())), preferred_element_type=jnp.float32)


def mm_t(left, right):
    return lax.dot_general(left, right, (((1,), (1,)), ((), ())), preferred_element_type=jnp.float32)


def kernel(
    tiles, groups, rim, field_hbm, interp_hbm, blocks_hbm, lists, result,
    field, interp, blocks, ip, conv, gram, base,
    edge_out, edge_in, slot_out, slot_in, back_out, back_in, part_out, part_in,
    load_sem, edge_send, edge_recv, slot_send, slot_recv, back_send, back_recv,
    part_send, part_recv,
):
    rows, columns = field.shape
    extended, points = interp.shape
    owned, bands, size = blocks.shape[0], blocks.shape[1], blocks.shape[2]
    slots = owned * size
    capacity = slots // groups
    height = rows // CHUNKS
    tile, me = lax.axis_index("tile"), lax.axis_index("conv")
    count = tiles * groups
    place = tile * groups + me
    after, before = lax.rem(place + 1, count), lax.rem(place + count - 1, count)
    right = (lax.div(after, groups), lax.rem(after, groups))
    left = (lax.div(before, groups), lax.rem(before, groups))
    hops = [groups // 2] + [k for k in range(1, groups) if k != groups // 2]
    peers = [lax.rem(me + k, groups) for k in hops]

    barrier = pltpu.get_barrier_semaphore()
    for other in [left, right] + [(tile, peer) for peer in peers]:
        pl.semaphore_signal(barrier, inc=1, device_id=other, device_id_type=MESH)

    def load(source, target, index):
        copy = pltpu.make_async_copy(source, target, load_sem.at[index])
        copy.start()
        return copy

    inner = slice(rim, columns - rim)
    lead, tail = slice(0, rim), slice(columns - rim, columns)
    load_lead = load(field_hbm.at[:, lead], field.at[:, lead], 1)
    load_tail = load(field_hbm.at[:, tail], field.at[:, tail], 2)
    load_interp = load(interp_hbm, interp, 4)
    load_inner = load(field_hbm.at[:, inner], field.at[:, inner], 5)
    load_blocks = load(blocks_hbm, blocks, 6)

    def piece(chunk):
        return slice(chunk * height, (chunk + 1) * height)

    def pair(send, recv, out_ref, in_ref, chunk, side, target):
        return pltpu.make_async_remote_copy(
            src_ref=out_ref.at[chunk, side], dst_ref=in_ref.at[chunk, side],
            send_sem=send.at[chunk, side], recv_sem=recv.at[chunk, side],
            device_id=target, device_id_type=MESH,
        )

    def exchange(send, recv, out_ref, in_ref, chunk):
        copies = []
        for peer in peers:
            copies.append(pltpu.make_async_remote_copy(
                src_ref=out_ref.at[chunk, peer], dst_ref=in_ref.at[chunk, me],
                send_sem=send.at[chunk, peer], recv_sem=recv.at[chunk, me],
                device_id=(tile, peer), device_id_type=MESH,
            ))
            copies[-1].start()
        in_ref[chunk, me] = out_ref[chunk, me]
        return copies

    def arrived(send, recv, out_ref, in_ref, chunk):
        for peer in peers:
            pltpu.make_async_remote_copy(
                src_ref=out_ref.at[chunk, peer], dst_ref=in_ref.at[chunk, peer],
                send_sem=send.at[chunk, peer], recv_sem=recv.at[chunk, peer],
                device_id=(tile, peer), device_id_type=MESH,
            ).wait_recv()
        return jnp.concatenate([in_ref[chunk, g] for g in range(groups)], axis=1)

    left_list = lists[:, points : points + rim]
    right_list = lists[:, points + rim : points + 2 * rim]
    lines = lax.broadcasted_iota(jnp.int32, (rim, rim), 0)
    left_pick = (lines == left_list).astype(jnp.float32).astype(jnp.bfloat16)
    right_pick = (lines + (columns - rim) == right_list).astype(jnp.float32).astype(jnp.bfloat16)
    load_lead.wait()
    load_tail.wait()
    for chunk in range(CHUNKS):
        part = piece(chunk)
        edge_out[chunk, 0] = mm(field[part, tail].astype(jnp.bfloat16), right_pick).astype(jnp.bfloat16)
        edge_out[chunk, 1] = mm(field[part, lead].astype(jnp.bfloat16), left_pick).astype(jnp.bfloat16)
    pl.semaphore_wait(barrier, 2 + len(peers))
    edge_copies, part_copies, slot_copies, back_copies = [], [], [], []
    for chunk in range(CHUNKS):
        for side, target in ((0, right), (1, left)):
            copy = pair(edge_send, edge_recv, edge_out, edge_in, chunk, side, target)
            copy.start()
            edge_copies.append(copy)

    owners = lists[:, 0:points]
    choose = (owners == lax.broadcasted_iota(jnp.int32, (-(-groups // 8) * 8, points), 0)).astype(jnp.float32)
    order = lax.broadcasted_iota(jnp.int32, (points, points), 0) < lax.broadcasted_iota(
        jnp.int32, (points, points), 1
    )
    ranks = mm(choose.astype(jnp.bfloat16), order.astype(jnp.float32).astype(jnp.bfloat16))
    rank = jnp.sum(ranks * choose, axis=0, keepdims=True)
    slot = owners * capacity + rank.astype(jnp.int32)
    placement = (slot == lax.broadcasted_iota(jnp.int32, (slots, points), 0)).astype(jnp.float32)
    placement = placement.astype(jnp.bfloat16)
    load_interp.wait()
    ip[0:rim, :] = mm_t(interp[0:rim, :], placement).astype(jnp.bfloat16)
    ip[rim : 2 * rim, :] = mm_t(interp[extended - rim :, :], placement).astype(jnp.bfloat16)
    ip[2 * rim :, :] = mm_t(interp[rim : extended - rim, :], placement).astype(jnp.bfloat16)
    load_inner.wait()
    base[...] = mm(field[...].astype(jnp.bfloat16), ip[2 * rim :, :])

    load_blocks.wait()
    for j in range(owned):
        for s in range(owned):
            total = jnp.zeros((size, size), jnp.float32)
            for c in range(bands):
                at = points + 2 * rim + j * bands + c
                reads = lax.rem(j + lists[:, at : at + 1], owned) == s
                total = total + jnp.where(reads, 1.0, 0.0) * blocks[j, c].astype(jnp.float32)
            conv[s * size : (s + 1) * size, j * size : (j + 1) * size] = total.astype(jnp.bfloat16)
    gram[...] = mm_t(conv[...], conv[...]).astype(jnp.bfloat16)

    for chunk in range(CHUNKS):
        for side, target in ((0, right), (1, left)):
            pair(edge_send, edge_recv, edge_out, edge_in, chunk, side, target).wait_recv()
        edges = jnp.concatenate([edge_in[chunk, 0], edge_in[chunk, 1]], axis=1)
        subgrid = (base[piece(chunk), :] + mm(edges, ip[0 : 2 * rim, :])).astype(jnp.bfloat16)
        for g in range(groups):
            slot_out[chunk, g] = subgrid[:, g * capacity : (g + 1) * capacity]
        slot_copies += exchange(slot_send, slot_recv, slot_out, slot_in, chunk)

    for chunk in range(CHUNKS):
        gathered = arrived(slot_send, slot_recv, slot_out, slot_in, chunk)
        adjoint = mm(gathered, gram[...]).astype(jnp.bfloat16)
        for g in range(groups):
            back_out[chunk, g] = adjoint[:, g * capacity : (g + 1) * capacity]
        back_copies += exchange(back_send, back_recv, back_out, back_in, chunk)

    for chunk in range(CHUNKS):
        part = piece(chunk)
        returned = arrived(back_send, back_recv, back_out, back_in, chunk)
        rims = mm_t(returned, ip[0 : 2 * rim, :]).astype(jnp.bfloat16)
        part_out[chunk, 0] = rims[:, rim:]
        part_out[chunk, 1] = rims[:, :rim]
        for side, target in ((0, right), (1, left)):
            copy = pair(part_send, part_recv, part_out, part_in, chunk, side, target)
            copy.start()
            part_copies.append(copy)
        result[part, :] = mm_t(returned, ip[2 * rim :, :])

    for chunk in range(CHUNKS):
        part = piece(chunk)
        for side, where, pick, target in ((0, lead, left_pick, right), (1, tail, right_pick, left)):
            pair(part_send, part_recv, part_out, part_in, chunk, side, target).wait_recv()
            result[part, where] += mm_t(part_in[chunk, side], pick)
    for copy in edge_copies + slot_copies + back_copies + part_copies:
        copy.wait_send()


def on_device(tiles, groups, field, interp, conv_blocks, band_shift, owner, edge_index):
    rows, columns = field.shape
    extended, points = interp.shape
    rim = edge_index.shape[1]
    slots = conv_blocks.shape[0] * conv_blocks.shape[2]
    capacity = slots // groups
    height = rows // CHUNKS
    half, single = jnp.bfloat16, jnp.float32
    sides = pltpu.VMEM((CHUNKS, 2, height, rim), half)
    cells = pltpu.VMEM((CHUNKS, groups, height, capacity), half)
    two, many = pltpu.SemaphoreType.DMA((CHUNKS, 2)), pltpu.SemaphoreType.DMA((CHUNKS, groups))
    lists = jnp.concatenate([owner.reshape(-1), edge_index.reshape(-1), band_shift.reshape(-1)])
    lists = jnp.pad(lists, (0, -lists.size % 128)).reshape(1, -1)
    anywhere = pl.BlockSpec(memory_space=pl.ANY)
    return pl.pallas_call(
        functools.partial(kernel, tiles, groups, rim),
        out_shape=jax.ShapeDtypeStruct(field.shape, single),
        in_specs=[anywhere] * 3 + [pl.BlockSpec(memory_space=pltpu.VMEM)],
        out_specs=pl.BlockSpec(memory_space=pltpu.VMEM),
        scratch_shapes=[
            pltpu.VMEM(field.shape, single),
            pltpu.VMEM(interp.shape, half),
            pltpu.VMEM(conv_blocks.shape, half),
            pltpu.VMEM((extended, slots), half),
            pltpu.VMEM((slots, slots), half),
            pltpu.VMEM((slots, slots), half),
            pltpu.VMEM((rows, slots), single),
            sides, sides, cells, cells, cells, cells, sides, sides,
            pltpu.SemaphoreType.DMA((7,)),
            two, two, many, many, many, many, two, two,
        ],
        compiler_params=pltpu.CompilerParams(collective_id=0, has_side_effects=True, vmem_limit_bytes=53 * 2**20),
    )(field, interp, conv_blocks, lists)


def solution(mesh):
    return jax.shard_map(
        functools.partial(on_device, mesh.shape["tile"], mesh.shape["conv"]),
        mesh=mesh,
        in_specs=(
            P(None, ("tile", "conv")),
            P(("tile", "conv"), None),
            P(("tile", "conv"), None, None, None),
            P(("tile", "conv"), None),
            P(("tile", "conv"), None),
            P(("tile", "conv"), None),
        ),
        out_specs=P(None, ("tile", "conv")),
        check_vma=False,
    )
```

profile of v0, /device:TPU:0, one launch (start us, length us, event | category | flops | bytes accessed | tf_op | source)
XLA Modules:
  0.0 25.9 jit_solution(1134368827948659442)
XLA Ops:
  0.0 0.0 copy-start
  0.0 0.8 %reshape.14 = s32[6]{0:T(128)S(1)} reshape(s32[2,3]{1,0:T(2,128)} %param.9) | data formatting | bytes 48 | tf_op jit(solution)/shard_map/reshape | solution.py:187
  0.8 0.0 copy-done
  0.8 0.0 copy-start.1
  0.8 0.7 %copy-done.1 = s32[2,128]{1,0:T(2,128)S(1)} copy-done((s32[2,128]{1,0:T(2,128)S(1)}, s32[2,128]{1,0:T(2,128)}, u32[]{:S(2)}) %copy-start.1) | copy-done | bytes 1048
  1.5 23.6 %shard_map.64 = f32[256,768]{1,0:T(8,128)S(1)} custom-call(f32[256,768]{1,0:T(8,128)} %field_hbm.1, bf16[1024,384]{1,0:T(8,128)(2,1)} %interp_hbm.1, bf16[2,3,256,256]{3,2,1,0:T(8,128)(2,1)} %blocks_hbm.1, s32[1,768]{1,0:T(1,128)S(1)} %reshape.15.lists), custom_call_target="tpu_custom_call" | custom-call | tf_op jit(solution)/shard_map/pallas_call | solution.py:190
  25.1 0.9 %copy.8 = f32[256,768]{1,0:T(8,128)} copy(f32[256,768]{1,0:T(8,128)S(1)} %shard_map.64) | data formatting | bytes 1572864
  (4 shorter events, 0.0 us)
Async XLA Ops:
  0.0 0.8 %copy-start = (s32[384,1]{0,1:T(1,128)S(1)}, s32[384,1]{0,1:T(1,128)}, u32[]{:S(2)}) copy-start(s32[384,1]{0,1:T(1,128)} %param.10) | copy-start | bytes 4612
  0.8 0.7 %copy-start.1 = (s32[2,128]{1,0:T(2,128)S(1)}, s32[2,128]{1,0:T(2,128)}, u32[]{:S(2)}) copy-start(s32[2,128]{1,0:T(2,128)} %param.11) | copy-start | bytes 3076
where the time goes:
time: 26.1 us; the launch traced here: 25.9 us
  Pallas kernels  23.6 us (90%)
  local copies, waits for them, and re-layouts  2.33 us (9%)
    pallas_call x1, Pallas kernels, on_device(): pl.pallas_call(functools.partial(kernel, tiles, groups, rim), out_shape=j...  23.6 us
    unnamed x5, local copies, waits for them, and re-layouts  1.54 us
    reshape x1, local copies, waits for them, and re-layouts, on_device(): band_shift.reshape(-1)  0.77 us

commit v1 on v0

v1 whole, which is shorter than its diff:
```python
import functools

import jax
import jax.numpy as jnp
from jax import lax
from jax.experimental import pallas as pl
from jax.experimental.pallas import tpu as pltpu
from jax.sharding import PartitionSpec as P

MESH = pl.DeviceIdType.MESH
CHUNKS = 2


def mm(left, right):
    return lax.dot_general(left, right, (((1,), (0,)), ((), ())), preferred_element_type=jnp.float32)


def mm_t(left, right):
    return lax.dot_general(left, right, (((1,), (1,)), ((), ())), preferred_element_type=jnp.float32)


def kernel(
    tiles, groups, rim, field_hbm, interp_hbm, blocks_hbm, owner_hbm, index_hbm, shift_hbm, result,
    field, interp, blocks, owner, index, shift, ip, conv, gram, base,
    edge_out, edge_in, late_in, rim_out, rim_in, cell_out, slot_in, back_in, far_out, far_in, part_out, part_in,
    load_sem, send_sem, edge_recv, late_recv, rim_recv, slot_recv, back_recv, part_recv,
):
    rows, columns = field.shape
    extended, points = interp.shape
    owned, bands, size = blocks.shape[0], blocks.shape[1], blocks.shape[2]
    slots = owned * size
    capacity = slots // groups
    height = rows // CHUNKS
    last = groups - 1
    tile, me = lax.axis_index("tile"), lax.axis_index("conv")
    after, before = lax.rem(tile + 1, tiles), lax.rem(tile + tiles - 1, tiles)
    up, down = lax.rem(me + 1, groups), lax.rem(me + last, groups)
    hops = [groups // 2] + [k for k in range(1, groups) if k != groups // 2]
    peers = [lax.rem(me + k, groups) for k in hops]

    barrier = pltpu.get_barrier_semaphore()

    def greet(target):
        pl.semaphore_signal(barrier, inc=1, device_id=target, device_id_type=MESH)

    greet((before, last))
    greet((after, 0))

    @pl.when(me == 0)
    def _():
        for g in range(last):
            greet((before, g))

    @pl.when(me == last)
    def _():
        for g in range(1, groups):
            greet((after, g))

    for peer in peers:
        greet((tile, peer))

    def load(source, target, at):
        copy = pltpu.make_async_copy(source, target, load_sem.at[at])
        copy.start()
        return copy

    def drain(ref, semaphore):
        pltpu.make_async_copy(ref, ref, semaphore).wait()

    inner = slice(rim, columns - rim)
    lead, tail = slice(0, rim), slice(columns - rim, columns)
    load_index = load(index_hbm, index, 0)
    load_lead = load(field_hbm.at[:, lead], field.at[:, lead], 1)
    load_tail = load(field_hbm.at[:, tail], field.at[:, tail], 2)
    load_owner = load(owner_hbm, owner, 3)
    load_interp = load(interp_hbm, interp, 4)
    load_inner = load(field_hbm.at[:, inner], field.at[:, inner], 5)
    load_shift = load(shift_hbm, shift, 6)
    load_blocks = load(blocks_hbm, blocks, 7)

    def piece(chunk):
        return slice(chunk * height, (chunk + 1) * height)

    def send(source, target, kind, arrival, place):
        pltpu.make_async_remote_copy(
            src_ref=source, dst_ref=target, send_sem=send_sem.at[kind], recv_sem=arrival,
            device_id=place, device_id_type=MESH,
        ).start()

    def exchange(kind, chunk, in_ref, recv):
        for peer in peers:
            send(cell_out.at[kind, chunk, peer], in_ref.at[chunk, me], 0, recv.at[chunk], (tile, peer))
        in_ref[chunk, me] = cell_out[kind, chunk, me]

    def arrived(chunk, in_ref, recv):
        drain(in_ref.at[chunk, 0:last], recv.at[chunk])
        return [in_ref[chunk, g] for g in range(groups)]

    load_index.wait()
    left_list, right_list = index[0:1, :], index[1:2, :]
    lines = lax.broadcasted_iota(jnp.int32, (rim, rim), 0)
    left_pick = (lines == left_list).astype(jnp.float32).astype(jnp.bfloat16)
    right_pick = (lines + (columns - rim) == right_list).astype(jnp.float32).astype(jnp.bfloat16)
    load_lead.wait()
    load_tail.wait()
    for chunk in range(CHUNKS):
        part = piece(chunk)
        edge_out[chunk, 0] = mm(field[part, tail].astype(jnp.bfloat16), right_pick).astype(jnp.bfloat16)
        edge_out[chunk, 1] = mm(field[part, lead].astype(jnp.bfloat16), left_pick).astype(jnp.bfloat16)

    load_owner.wait()
    owners = owner[...]
    choose = (owners == lax.broadcasted_iota(jnp.int32, (-(-groups // 8) * 8, points), 0)).astype(jnp.float32)
    order = lax.broadcasted_iota(jnp.int32, (points, points), 0) < lax.broadcasted_iota(
        jnp.int32, (points, points), 1
    )
    ranks = mm(choose.astype(jnp.bfloat16), order.astype(jnp.float32).astype(jnp.bfloat16))
    rank = jnp.sum(ranks * choose, axis=0, keepdims=True)
    slot = owners * capacity + rank.astype(jnp.int32)
    placement = (slot == lax.broadcasted_iota(jnp.int32, (slots, points), 0)).astype(jnp.float32)
    placement = placement.astype(jnp.bfloat16)
    load_interp.wait()
    ip[0:rim, :] = mm_t(interp[0:rim, :], placement).astype(jnp.bfloat16)
    ip[rim : 2 * rim, :] = mm_t(interp[extended - rim :, :], placement).astype(jnp.bfloat16)

    def share(side, at):
        for g in range(groups):
            rim_out[g] = ip[side * rim : (side + 1) * rim, g * capacity : (g + 1) * capacity]
        rim_in[side] = rim_out[at]
        for chunk in range(CHUNKS):
            edge_in[chunk, side] = jnp.zeros((height, rim), jnp.bfloat16)

    pl.when(me == 0)(functools.partial(share, 0, 0))
    pl.when(me == last)(functools.partial(share, 1, last))

    pl.semaphore_wait(barrier, jnp.where((me == 0) | (me == last), 2 * groups, last + 2))

    for chunk in range(CHUNKS):

        @pl.when(me == 0)
        def _():
            for g in range(groups):
                send(edge_out.at[chunk, 1], late_in.at[chunk, 1], 1, late_recv.at[chunk], (before, g))

        @pl.when(me == last)
        def _():
            for g in range(groups):
                send(edge_out.at[chunk, 0], late_in.at[chunk, 0], 1, late_recv.at[chunk], (after, g))

        @pl.when(me < last)
        def _():
            send(edge_out.at[chunk, 0], edge_in.at[chunk, 0], 2, edge_recv.at[chunk, 0], (tile, up))

        @pl.when(me > 0)
        def _():
            send(edge_out.at[chunk, 1], edge_in.at[chunk, 1], 2, edge_recv.at[chunk, 1], (tile, down))

    @pl.when(me == 0)
    def _():
        for g in range(1, groups):
            send(rim_out.at[g], rim_in.at[0], 3, rim_recv.at[0], (tile, g))

    @pl.when(me == last)
    def _():
        for g in range(last):
            send(rim_out.at[g], rim_in.at[1], 3, rim_recv.at[1], (tile, g))

    ip[2 * rim :, :] = mm_t(interp[rim : extended - rim, :], placement).astype(jnp.bfloat16)
    load_inner.wait()
    base[...] = mm(field[...].astype(jnp.bfloat16), ip[2 * rim :, :])

    load_shift.wait()
    load_blocks.wait()
    for j in range(owned):
        for s in range(owned):
            total = jnp.zeros((size, size), jnp.float32)
            for c in range(bands):
                reads = lax.rem(j + shift[j : j + 1, c : c + 1], owned) == s
                total = total + jnp.where(reads, 1.0, 0.0) * blocks[j, c].astype(jnp.float32)
            conv[s * size : (s + 1) * size, j * size : (j + 1) * size] = total.astype(jnp.bfloat16)
    gram[...] = mm_t(conv[...], conv[...]).astype(jnp.bfloat16)

    for chunk in range(CHUNKS):
        pl.when(me > 0)(lambda: drain(edge_in.at[chunk, 0], edge_recv.at[chunk, 0]))
        pl.when(me < last)(lambda: drain(edge_in.at[chunk, 1], edge_recv.at[chunk, 1]))
        edges = jnp.concatenate([edge_in[chunk, 0], edge_in[chunk, 1]], axis=1)
        subgrid = (base[piece(chunk), :] + mm(edges, ip[0 : 2 * rim, :])).astype(jnp.bfloat16)
        for g in range(groups):
            cell_out[0, chunk, g] = subgrid[:, g * capacity : (g + 1) * capacity]
        exchange(0, chunk, slot_in, slot_recv)

    pl.when(me > 0)(lambda: drain(rim_in.at[0], rim_recv.at[0]))
    pl.when(me < last)(lambda: drain(rim_in.at[1], rim_recv.at[1]))
    for chunk in range(CHUNKS):
        cells = arrived(chunk, slot_in, slot_recv)
        drain(late_in.at[chunk], late_recv.at[chunk])
        for side, g in ((0, 0), (1, last)):
            cells[g] = (cells[g].astype(jnp.float32) + mm(late_in[chunk, side], rim_in[side])).astype(jnp.bfloat16)
        adjoint = mm(jnp.concatenate(cells, axis=1), gram[...]).astype(jnp.bfloat16)
        for g in range(groups):
            cell_out[1, chunk, g] = adjoint[:, g * capacity : (g + 1) * capacity]
        exchange(1, chunk, back_in, back_recv)
        for side, g in ((0, 0), (1, last)):
            far_out[chunk, side] = mm_t(cell_out[1, chunk, g], rim_in[side]).astype(jnp.bfloat16)
        send(far_out.at[chunk, 0], far_in.at[chunk, me], 4, part_recv.at[chunk, 1], (before, last))
        send(far_out.at[chunk, 1], far_in.at[chunk, me], 4, part_recv.at[chunk, 0], (after, 0))

    for chunk in range(CHUNKS):
        part = piece(chunk)
        returned = jnp.concatenate(arrived(chunk, back_in, back_recv), axis=1)
        rims = mm_t(returned, ip[0 : 2 * rim, :]).astype(jnp.bfloat16)
        part_out[chunk, 0] = rims[:, rim:]
        part_out[chunk, 1] = rims[:, :rim]

        @pl.when(me < last)
        def _():
            send(part_out.at[chunk, 0], part_in.at[chunk, 0], 5, part_recv.at[chunk, 0], (tile, up))

        @pl.when(me > 0)
        def _():
            send(part_out.at[chunk, 1], part_in.at[chunk, 1], 5, part_recv.at[chunk, 1], (tile, down))

        result[part, :] = mm_t(returned, ip[2 * rim :, :])

    for chunk in range(CHUNKS):
        part = piece(chunk)
        for side, where, pick, end in ((0, lead, left_pick, 0), (1, tail, right_pick, last)):

            @pl.when(me != end)
            def _():
                drain(part_in.at[chunk, side], part_recv.at[chunk, side])
                result[part, where] += mm_t(part_in[chunk, side], pick)

            @pl.when(me == end)
            def _():
                drain(far_in.at[chunk], part_recv.at[chunk, side])
                total = result[part, where]
                for g in range(groups):
                    total = total + mm_t(far_in[chunk, g], pick)
                result[part, where] = total

    drain(cell_out.at[:, :, 0:last], send_sem.at[0])
    drain(far_out, send_sem.at[4])

    @pl.when((me == 0) | (me == last))
    def _():
        drain(far_in, send_sem.at[1])
        drain(edge_out.at[:, 0], send_sem.at[2])
        drain(rim_out.at[0:last], send_sem.at[3])
        drain(part_out.at[:, 0], send_sem.at[5])

    @pl.when((me != 0) & (me != last))
    def _():
        drain(edge_out, send_sem.at[2])
        drain(part_out, send_sem.at[5])


def in_hbm(array):
    return pltpu.with_memory_space_constraint(array, pltpu.HBM)


def on_device(tiles, groups, field, interp, conv_blocks, band_shift, owner, edge_index):
    rows, columns = field.shape
    extended, points = interp.shape
    rim = edge_index.shape[1]
    slots = conv_blocks.shape[0] * conv_blocks.shape[2]
    capacity = slots // groups
    height = rows // CHUNKS
    half, single = jnp.bfloat16, jnp.float32
    sides = pltpu.VMEM((CHUNKS, 2, height, rim), half)
    cells = pltpu.VMEM((CHUNKS, groups, height, capacity), half)
    dma = pltpu.SemaphoreType.DMA
    anywhere = pl.BlockSpec(memory_space=pltpu.HBM)
    return pl.pallas_call(
        functools.partial(kernel, tiles, groups, rim),
        out_shape=jax.ShapeDtypeStruct(field.shape, single),
        in_specs=[anywhere] * 6,
        out_specs=pl.BlockSpec(memory_space=pltpu.VMEM),
        scratch_shapes=[
            pltpu.VMEM(field.shape, single),
            pltpu.VMEM(interp.shape, half),
            pltpu.VMEM(conv_blocks.shape, half),
            pltpu.VMEM((1, points), jnp.int32),
            pltpu.VMEM(edge_index.shape, jnp.int32),
            pltpu.VMEM(band_shift.shape, jnp.int32),
            pltpu.VMEM((extended, slots), half),
            pltpu.VMEM((slots, slots), half),
            pltpu.VMEM((slots, slots), half),
            pltpu.VMEM((rows, slots), single),
            sides, sides, sides,
            pltpu.VMEM((groups, rim, capacity), half),
            pltpu.VMEM((2, rim, capacity), half),
            pltpu.VMEM((2, CHUNKS, groups, height, capacity), half),
            cells, cells,
            sides,
            pltpu.VMEM((CHUNKS, groups, height, rim), half),
            sides, sides,
            dma((8,)), dma((6,)), dma((CHUNKS, 2)), dma((CHUNKS,)), dma((2,)), dma((CHUNKS,)), dma((CHUNKS,)),
            dma((CHUNKS, 2)),
        ],
        compiler_params=pltpu.CompilerParams(collective_id=0, has_side_effects=True, vmem_limit_bytes=53 * 2**20),
    )(field, interp, conv_blocks, *[in_hbm(small) for small in (owner.reshape(1, -1), edge_index, band_shift)])


def solution(mesh):
    return jax.shard_map(
        functools.partial(on_device, mesh.shape["tile"], mesh.shape["conv"]),
        mesh=mesh,
        in_specs=(
            P(None, ("tile", "conv")),
            P(("tile", "conv"), None),
            P(("tile", "conv"), None, None, None),
            P(("tile", "conv"), None),
            P(("tile", "conv"), None),
            P(("tile", "conv"), None),
        ),
        out_specs=P(None, ("tile", "conv")),
        check_vma=False,
    )
```

time: 26.1 us -> 22.4 us (0.86)
  Pallas kernels: 23.6 us -> 21.1 us
  local copies, waits for them, and re-layouts: 2.33 us -> 0.88 us
    pallas_call x1, Pallas kernels: 23.6 us -> 21.1 us  [on_device(): pl.pallas_call(functools.partial(kernel, tiles, groups, rim), out_shape=j...]
    reshape x2 -> x0, local copies, waits for them, and re-layouts: 0.78 us -> none  [the longest x1 0.77 us: on_device(): band_shift.reshape(-1)]
    unnamed x5 -> x1, local copies, waits for them, and re-layouts: 1.54 us -> 0.88 us
where the time goes in v1:
time: 22.4 us; the launch traced here: 22 us
  Pallas kernels  21.1 us (94%)
  local copies, waits for them, and re-layouts  0.88 us (4%)
    pallas_call x1, Pallas kernels, on_device(): pl.pallas_call(functools.partial(kernel, tiles, groups, rim), out_shape=j...  21.1 us
    unnamed x1, local copies, waits for them, and re-layouts  0.88 us

profile of v1, /device:TPU:0, one launch (start us, length us, event | category | flops | bytes accessed | tf_op | source)
XLA Modules:
  0.0 22.0 jit_solution(14142422457214164471)
XLA Ops:
  0.0 21.1 %shard_map.64 = f32[256,768]{1,0:T(8,128)S(1)} custom-call(f32[256,768]{1,0:T(8,128)} %field_hbm.1, bf16[1024,384]{1,0:T(8,128)(2,1)} %interp_hbm.1, bf16[2,3,256,256]{3,2,1,0:T(8,128)(2,1)} %blocks_hbm.1, s32[1,384]{1,0:T(1,128)} %bitcast.1, s32[2,128]{1,0:T(2,128)} %index_hbm.1, s32[2,3]{1,0:T(2,128)} %shift_hbm.1), custom_call_target="tpu_custom_call" | custom-call | tf_op jit(solution)/shard_map/pallas_call | solution.py:274
  21.1 0.9 %copy.8 = f32[256,768]{1,0:T(8,128)} copy(f32[256,768]{1,0:T(8,128)S(1)} %shard_map.64) | data formatting | bytes 1572864

commit v2 on v1

--- a/solution.py
+++ b/solution.py
@@ -22,8 +22,8 @@
 def kernel(
     tiles, groups, rim, field_hbm, interp_hbm, blocks_hbm, owner_hbm, index_hbm, shift_hbm, result,
     field, interp, blocks, owner, index, shift, ip, conv, gram, base,
-    edge_out, edge_in, late_in, rim_out, rim_in, cell_out, slot_in, back_in, far_out, far_in, part_out, part_in,
-    load_sem, send_sem, edge_recv, late_recv, rim_recv, slot_recv, back_recv, part_recv,
+    edge_out, edge_in, relay, late_in, rim_out, rim_in, cell_out, slot_in, back_in, share, share_out, share_in, far_out, far_in, part_out, part_in,
+    ready, load_sem, send_sem, edge_recv, relay_recv, late_recv, rim_recv, slot_recv, back_recv, share_recv, part_recv,
 ):
     rows, columns = field.shape
     extended, points = interp.shape
@@ -39,25 +39,36 @@
     peers = [lax.rem(me + k, groups) for k in hops]
 
     barrier = pltpu.get_barrier_semaphore()
-
-    def greet(target):
-        pl.semaphore_signal(barrier, inc=1, device_id=target, device_id_type=MESH)
-
-    greet((before, last))
-    greet((after, 0))
-
-    @pl.when(me == 0)
-    def _():
-        for g in range(last):
-            greet((before, g))
-
-    @pl.when(me == last)
-    def _():
-        for g in range(1, groups):
-            greet((after, g))
-
+    first_tile, last_tile = tile == 0, tile == tiles - 1
+    odd = lax.rem(me, 2)
+    even = odd == 0
+    mate = me + 1 - 2 * odd
+
+    def meet(lower, upper):
+        return (upper == 0) | (lower == last) | (upper == lower - lax.rem(lower, 2))
+
+    with_before = [meet(g, me) for g in range(groups)]
+    with_after = [meet(me, g) for g in range(groups)]
+    from_before = sum(jnp.where(met, 1, 0) for met in with_before)
+    from_after = sum(jnp.where(met, 1, 0) for met in with_after)
+
+    def signal(semaphore, target):
+        pl.semaphore_signal(semaphore, inc=1, device_id=target, device_id_type=MESH)
+
+    def tell(semaphore, there, met):
+        for g in range(groups):
+            pl.when(met[g])(functools.partial(signal, semaphore, (there, g)))
+
+    def tell_before(semaphore):
+        tell(semaphore, before, with_before)
+
+    def tell_after(semaphore):
+        tell(semaphore, after, with_after)
+
+    pl.when(first_tile)(lambda: tell_before(barrier))
+    pl.when(~last_tile)(lambda: tell_after(barrier))
     for peer in peers:
-        greet((tile, peer))
+        signal(barrier, (tile, peer))
 
     def load(source, target, at):
         copy = pltpu.make_async_copy(source, target, load_sem.at[at])
@@ -96,6 +107,12 @@
         drain(in_ref.at[chunk, 0:last], recv.at[chunk])
         return [in_ref[chunk, g] for g in range(groups)]
 
+    pl.semaphore_wait(
+        barrier, last + jnp.where(first_tile, 0, from_before) + jnp.where(last_tile, from_after, 0)
+    )
+    pl.when(~first_tile)(lambda: tell_before(ready.at[1]))
+    pl.when(last_tile)(lambda: tell_after(ready.at[0]))
+
     load_index.wait()
     left_list, right_list = index[0:1, :], index[1:2, :]
     lines = lax.broadcasted_iota(jnp.int32, (rim, rim), 0)
@@ -107,6 +124,29 @@
         part = piece(chunk)
         edge_out[chunk, 0] = mm(field[part, tail].astype(jnp.bfloat16), right_pick).astype(jnp.bfloat16)
         edge_out[chunk, 1] = mm(field[part, lead].astype(jnp.bfloat16), left_pick).astype(jnp.bfloat16)
+
+    for chunk in range(CHUNKS):
+
+        @pl.when(me < last)
+        def _():
+            send(edge_out.at[chunk, 0], edge_in.at[chunk, 0], 2, edge_recv.at[chunk, 0], (tile, up))
+
+        @pl.when(me > 0)
+        def _():
+            send(edge_out.at[chunk, 1], edge_in.at[chunk, 1], 2, edge_recv.at[chunk, 1], (tile, down))
+
+    @pl.when(me == 0)
+    def _():
+        relay[...] = edge_out[:, 1]
+        for g in range(2, groups, 2):
+            send(edge_out.at[:, 1], relay, 6, relay_recv.at[0], (tile, g))
+
+    def late_right():
+        for chunk in range(CHUNKS):
+            for g in range(1, groups, 2):
+                send(edge_out.at[chunk, 0], late_in.at[chunk, 0], 1, late_recv.at[chunk, 0], (after, g))
+
+    pl.when((me == last) & last_tile)(late_right)
 
     load_owner.wait()
     owners = owner[...]
@@ -123,37 +163,15 @@
     ip[0:rim, :] = mm_t(interp[0:rim, :], placement).astype(jnp.bfloat16)
     ip[rim : 2 * rim, :] = mm_t(interp[extended - rim :, :], placement).astype(jnp.bfloat16)
 
-    def share(side, at):
+    def spread(side, at):
         for g in range(groups):
             rim_out[g] = ip[side * rim : (side + 1) * rim, g * capacity : (g + 1) * capacity]
         rim_in[side] = rim_out[at]
         for chunk in range(CHUNKS):
             edge_in[chunk, side] = jnp.zeros((height, rim), jnp.bfloat16)
 
-    pl.when(me == 0)(functools.partial(share, 0, 0))
-    pl.when(me == last)(functools.partial(share, 1, last))
-
-    pl.semaphore_wait(barrier, jnp.where((me == 0) | (me == last), 2 * groups, last + 2))
-
-    for chunk in range(CHUNKS):
-
-        @pl.when(me == 0)
-        def _():
-            for g in range(groups):
-                send(edge_out.at[chunk, 1], late_in.at[chunk, 1], 1, late_recv.at[chunk], (before, g))
-
-        @pl.when(me == last)
-        def _():
-            for g in range(groups):
-                send(edge_out.at[chunk, 0], late_in.at[chunk, 0], 1, late_recv.at[chunk], (after, g))
-
-        @pl.when(me < last)
-        def _():
-            send(edge_out.at[chunk, 0], edge_in.at[chunk, 0], 2, edge_recv.at[chunk, 0], (tile, up))
-
-        @pl.when(me > 0)
-        def _():
-            send(edge_out.at[chunk, 1], edge_in.at[chunk, 1], 2, edge_recv.at[chunk, 1], (tile, down))
+    pl.when(me == 0)(functools.partial(spread, 0, 0))
+    pl.when(me == last)(functools.partial(spread, 1, last))
 
     @pl.when(me == 0)
     def _():
@@ -168,6 +186,29 @@
     ip[2 * rim :, :] = mm_t(interp[rim : extended - rim, :], placement).astype(jnp.bfloat16)
     load_inner.wait()
     base[...] = mm(field[...].astype(jnp.bfloat16), ip[2 * rim :, :])
+
+    for chunk in range(CHUNKS):
+        pl.when(me > 0)(lambda: drain(edge_in.at[chunk, 0], edge_recv.at[chunk, 0]))
+        pl.when(me < last)(lambda: drain(edge_in.at[chunk, 1], edge_recv.at[chunk, 1]))
+        edges = jnp.concatenate([edge_in[chunk, 0], edge_in[chunk, 1]], axis=1)
+        subgrid = (base[piece(chunk), :] + mm(edges, ip[0 : 2 * rim, :])).astype(jnp.bfloat16)
+        for g in range(groups):
+            cell_out[0, chunk, g] = subgrid[:, g * capacity : (g + 1) * capacity]
+        exchange(0, chunk, slot_in, slot_recv)
+
+    @pl.when((me == last) & ~last_tile)
+    def _():
+        pl.semaphore_wait(ready.at[1], from_after)
+        late_right()
+
+    pl.when(even & (me != 0))(lambda: drain(relay, relay_recv.at[0]))
+
+    @pl.when(even)
+    def _():
+        pl.when(first_tile)(lambda: pl.semaphore_wait(ready.at[0], from_before))
+        for chunk in range(CHUNKS):
+            for g in (me, me + 1):
+                send(relay.at[chunk], late_in.at[chunk, 1], 1, late_recv.at[chunk, 1], (before, g))
 
     load_shift.wait()
     load_blocks.wait()
@@ -180,30 +221,43 @@
             conv[s * size : (s + 1) * size, j * size : (j + 1) * size] = total.astype(jnp.bfloat16)
     gram[...] = mm_t(conv[...], conv[...]).astype(jnp.bfloat16)
 
-    for chunk in range(CHUNKS):
-        pl.when(me > 0)(lambda: drain(edge_in.at[chunk, 0], edge_recv.at[chunk, 0]))
-        pl.when(me < last)(lambda: drain(edge_in.at[chunk, 1], edge_recv.at[chunk, 1]))
-        edges = jnp.concatenate([edge_in[chunk, 0], edge_in[chunk, 1]], axis=1)
-        subgrid = (base[piece(chunk), :] + mm(edges, ip[0 : 2 * rim, :])).astype(jnp.bfloat16)
-        for g in range(groups):
-            cell_out[0, chunk, g] = subgrid[:, g * capacity : (g + 1) * capacity]
-        exchange(0, chunk, slot_in, slot_recv)
-
     pl.when(me > 0)(lambda: drain(rim_in.at[0], rim_recv.at[0]))
     pl.when(me < last)(lambda: drain(rim_in.at[1], rim_recv.at[1]))
+    pl.when(~even & first_tile)(lambda: pl.semaphore_wait(ready.at[0], from_before))
+    pl.when((me != last) & ~last_tile)(lambda: pl.semaphore_wait(ready.at[1], from_after))
+
+    @pl.when(~even)
+    def _():
+        for chunk in range(CHUNKS):
+            drain(late_in.at[chunk, 0], late_recv.at[chunk, 0])
+            send(late_in.at[chunk, 0], late_in.at[chunk, 0], 8, late_recv.at[chunk, 0], (tile, mate))
+
     for chunk in range(CHUNKS):
         cells = arrived(chunk, slot_in, slot_recv)
-        drain(late_in.at[chunk], late_recv.at[chunk])
+        pl.when(even)(lambda: drain(late_in.at[chunk, 0], late_recv.at[chunk, 0]))
+        drain(late_in.at[chunk, 1], late_recv.at[chunk, 1])
         for side, g in ((0, 0), (1, last)):
             cells[g] = (cells[g].astype(jnp.float32) + mm(late_in[chunk, side], rim_in[side])).astype(jnp.bfloat16)
         adjoint = mm(jnp.concatenate(cells, axis=1), gram[...]).astype(jnp.bfloat16)
         for g in range(groups):
             cell_out[1, chunk, g] = adjoint[:, g * capacity : (g + 1) * capacity]
         exchange(1, chunk, back_in, back_recv)
-        for side, g in ((0, 0), (1, last)):
-            far_out[chunk, side] = mm_t(cell_out[1, chunk, g], rim_in[side]).astype(jnp.bfloat16)
-        send(far_out.at[chunk, 0], far_in.at[chunk, me], 4, part_recv.at[chunk, 1], (before, last))
-        send(far_out.at[chunk, 1], far_in.at[chunk, me], 4, part_recv.at[chunk, 0], (after, 0))
+        share_out[chunk] = mm_t(cell_out[1, chunk, (1 - odd) * last], rim_in[1 - odd]).astype(jnp.bfloat16)
+        send(share_out.at[chunk], share_in.at[chunk], 7, share_recv.at[chunk], (tile, mate))
+        share[chunk] = mm_t(cell_out[1, chunk, odd * last], rim_in[odd])
+
+    for chunk in range(CHUNKS):
+        drain(share_in.at[chunk], share_recv.at[chunk])
+        far_out[chunk] = (share[chunk] + share_in[chunk].astype(jnp.float32)).astype(jnp.bfloat16)
+        place = lax.div(me, 2)
+
+        @pl.when(even)
+        def _():
+            send(far_out.at[chunk], far_in.at[chunk, place], 4, part_recv.at[chunk, 1], (before, last))
+
+        @pl.when(~even)
+        def _():
+            send(far_out.at[chunk], far_in.at[chunk, place], 4, part_recv.at[chunk, 0], (after, 0))
 
     for chunk in range(CHUNKS):
         part = piece(chunk)
@@ -235,16 +289,21 @@
             def _():
                 drain(far_in.at[chunk], part_recv.at[chunk, side])
                 total = result[part, where]
-                for g in range(groups):
+                for g in range(groups // 2):
                     total = total + mm_t(far_in[chunk, g], pick)
                 result[part, where] = total
 
     drain(cell_out.at[:, :, 0:last], send_sem.at[0])
     drain(far_out, send_sem.at[4])
+    drain(share_out, send_sem.at[7])
+    pl.when(even)(lambda: drain(late_in, send_sem.at[1]))
+    pl.when(~even)(lambda: drain(late_in.at[:, 0], send_sem.at[8]))
+
+    pl.when(me == 0)(lambda: drain(far_in.at[:, 0 : groups // 2 - 1], send_sem.at[6]))
+    pl.when(me == last)(lambda: drain(far_in, send_sem.at[1]))
 
     @pl.when((me == 0) | (me == last))
     def _():
-        drain(far_in, send_sem.at[1])
         drain(edge_out.at[:, 0], send_sem.at[2])
         drain(rim_out.at[0:last], send_sem.at[3])
         drain(part_out.at[:, 0], send_sem.at[5])
@@ -268,6 +327,7 @@
     height = rows // CHUNKS
     half, single = jnp.bfloat16, jnp.float32
     sides = pltpu.VMEM((CHUNKS, 2, height, rim), half)
+    strip = pltpu.VMEM((CHUNKS, height, rim), half)
     cells = pltpu.VMEM((CHUNKS, groups, height, capacity), half)
     dma = pltpu.SemaphoreType.DMA
     anywhere = pl.BlockSpec(memory_space=pltpu.HBM)
@@ -287,15 +347,16 @@
             pltpu.VMEM((slots, slots), half),
             pltpu.VMEM((slots, slots), half),
             pltpu.VMEM((rows, slots), single),
-            sides, sides, sides,
+            sides, sides, strip, sides,
             pltpu.VMEM((groups, rim, capacity), half),
             pltpu.VMEM((2, rim, capacity), half),
             pltpu.VMEM((2, CHUNKS, groups, height, capacity), half),
             cells, cells,
-            sides,
-            pltpu.VMEM((CHUNKS, groups, height, rim), half),
+            pltpu.VMEM((CHUNKS, height, rim), single),
+            strip, strip, strip,
+            pltpu.VMEM((CHUNKS, groups // 2, height, rim), half),
             sides, sides,
-            dma((8,)), dma((6,)), dma((CHUNKS, 2)), dma((CHUNKS,)), dma((2,)), dma((CHUNKS,)), dma((CHUNKS,)),
+            pltpu.SemaphoreType.REGULAR((2,)), dma((8,)), dma((9,)), dma((CHUNKS, 2)), dma((1,)), dma((CHUNKS, 2)), dma((2,)), dma((CHUNKS,)), dma((CHUNKS,)), dma((CHUNKS,)),
             dma((CHUNKS, 2)),
         ],
         compiler_params=pltpu.CompilerParams(collective_id=0, has_side_effects=True, vmem_limit_bytes=53 * 2**20),

time: 22.4 us -> 20 us (0.89); the launches traced: 22 us -> 19.9 us
  Pallas kernels: 21.1 us -> 19 us
    pallas_call x1, Pallas kernels: 21.1 us -> 19 us  [on_device(): pl.pallas_call(functools.partial(kernel, tiles, groups, rim), out_shape=j...]
where the time goes in v2:
time: 20 us; the launch traced here: 19.9 us
  Pallas kernels  19 us (95%)
  local copies, waits for them, and re-layouts  0.88 us (4%)
    pallas_call x1, Pallas kernels, on_device(): pl.pallas_call(functools.partial(kernel, tiles, groups, rim), out_shape=j...  19 us
    unnamed x1, local copies, waits for them, and re-layouts  0.88 us

profile of v2, /device:TPU:0, one launch (start us, length us, event | category | flops | bytes accessed | tf_op | source)
XLA Modules:
  0.0 19.9 jit_solution(10071033142684184219)
XLA Ops:
  0.0 19.0 %shard_map.64 = f32[256,768]{1,0:T(8,128)S(1)} custom-call(f32[256,768]{1,0:T(8,128)} %field_hbm.1, bf16[1024,384]{1,0:T(8,128)(2,1)} %interp_hbm.1, bf16[2,3,256,256]{3,2,1,0:T(8,128)(2,1)} %blocks_hbm.1, s32[1,384]{1,0:T(1,128)} %bitcast.1, s32[2,128]{1,0:T(2,128)} %index_hbm.1, s32[2,3]{1,0:T(2,128)} %shift_hbm.1), custom_call_target="tpu_custom_call" | custom-call | tf_op jit(solution)/shard_map/pallas_call | solution.py:334
  19.0 0.9 %copy.8 = f32[256,768]{1,0:T(8,128)} copy(f32[256,768]{1,0:T(8,128)S(1)} %shard_map.64) | data formatting | bytes 1572864

commit v3 on v2

--- a/solution.py
+++ b/solution.py
@@ -22,7 +22,7 @@
 def kernel(
     tiles, groups, rim, field_hbm, interp_hbm, blocks_hbm, owner_hbm, index_hbm, shift_hbm, result,
     field, interp, blocks, owner, index, shift, ip, conv, gram, base,
-    edge_out, edge_in, relay, late_in, rim_out, rim_in, cell_out, slot_in, back_in, share, share_out, share_in, far_out, far_in, part_out, part_in,
+    edge_out, edge_in, relay, late_in, rim_out, rim_in, cell_out, slot_in, back_in, far_gram, share, share_in, far_out, far_in, part_out, part_in,
     ready, load_sem, send_sem, edge_recv, relay_recv, late_recv, rim_recv, slot_recv, back_recv, share_recv, part_recv,
 ):
     rows, columns = field.shape
@@ -35,8 +35,10 @@
     tile, me = lax.axis_index("tile"), lax.axis_index("conv")
     after, before = lax.rem(tile + 1, tiles), lax.rem(tile + tiles - 1, tiles)
     up, down = lax.rem(me + 1, groups), lax.rem(me + last, groups)
-    hops = [groups // 2] + [k for k in range(1, groups) if k != groups // 2]
-    peers = [lax.rem(me + k, groups) for k in hops]
+    middle = groups // 2
+    low = me < middle
+    peers = [jnp.where(low, middle + k, middle - 1 - k) for k in range(middle)]
+    peers += [lax.rem(me + k, middle) + jnp.where(low, 0, middle) for k in range(1, middle)]
 
     barrier = pltpu.get_barrier_semaphore()
     first_tile, last_tile = tile == 0, tile == tiles - 1
@@ -92,15 +94,15 @@
     def piece(chunk):
         return slice(chunk * height, (chunk + 1) * height)
 
-    def send(source, target, kind, arrival, place):
+    def send(source, target, arrival, place):
         pltpu.make_async_remote_copy(
-            src_ref=source, dst_ref=target, send_sem=send_sem.at[kind], recv_sem=arrival,
+            src_ref=source, dst_ref=target, send_sem=send_sem.at[0], recv_sem=arrival,
             device_id=place, device_id_type=MESH,
         ).start()
 
     def exchange(kind, chunk, in_ref, recv):
         for peer in peers:
-            send(cell_out.at[kind, chunk, peer], in_ref.at[chunk, me], 0, recv.at[chunk], (tile, peer))
+            send(cell_out.at[kind, chunk, peer], in_ref.at[chunk, me], recv.at[chunk], (tile, peer))
         in_ref[chunk, me] = cell_out[kind, chunk, me]
 
     def arrived(chunk, in_ref, recv):
@@ -129,22 +131,22 @@
 
         @pl.when(me < last)
         def _():
-            send(edge_out.at[chunk, 0], edge_in.at[chunk, 0], 2, edge_recv.at[chunk, 0], (tile, up))
+            send(edge_out.at[chunk, 0], edge_in.at[chunk, 0], edge_recv.at[chunk, 0], (tile, up))
 
         @pl.when(me > 0)
         def _():
-            send(edge_out.at[chunk, 1], edge_in.at[chunk, 1], 2, edge_recv.at[chunk, 1], (tile, down))
-
-    @pl.when(me == 0)
+            send(edge_out.at[chunk, 1], edge_in.at[chunk, 1], edge_recv.at[chunk, 1], (tile, down))
+
+    @pl.when((me == 0) & ~last_tile)
     def _():
         relay[...] = edge_out[:, 1]
         for g in range(2, groups, 2):
-            send(edge_out.at[:, 1], relay, 6, relay_recv.at[0], (tile, g))
+            send(edge_out.at[:, 1], relay, relay_recv.at[0], (tile, g))
 
     def late_right():
         for chunk in range(CHUNKS):
             for g in range(1, groups, 2):
-                send(edge_out.at[chunk, 0], late_in.at[chunk, 0], 1, late_recv.at[chunk, 0], (after, g))
+                send(edge_out.at[chunk, 0], late_in.at[chunk, 0], late_recv.at[chunk, 0], (after, g))
 
     pl.when((me == last) & last_tile)(late_right)
 
@@ -176,12 +178,12 @@
     @pl.when(me == 0)
     def _():
         for g in range(1, groups):
-            send(rim_out.at[g], rim_in.at[0], 3, rim_recv.at[0], (tile, g))
+            send(rim_out.at[g], rim_in.at[0], rim_recv.at[0], (tile, g))
 
     @pl.when(me == last)
     def _():
         for g in range(last):
-            send(rim_out.at[g], rim_in.at[1], 3, rim_recv.at[1], (tile, g))
+            send(rim_out.at[g], rim_in.at[1], rim_recv.at[1], (tile, g))
 
     ip[2 * rim :, :] = mm_t(interp[rim : extended - rim, :], placement).astype(jnp.bfloat16)
     load_inner.wait()
@@ -201,14 +203,18 @@
         pl.semaphore_wait(ready.at[1], from_after)
         late_right()
 
-    pl.when(even & (me != 0))(lambda: drain(relay, relay_recv.at[0]))
-
-    @pl.when(even)
+    def late_left(source, cores):
+        for chunk in range(CHUNKS):
+            for g in cores:
+                send(source.at[chunk], late_in.at[chunk, 1], late_recv.at[chunk, 1], (before, g))
+
+    pl.when(last_tile & (me == 0))(lambda: late_left(edge_out.at[:, 1], range(groups)))
+    pl.when(even & (me != 0) & ~last_tile)(lambda: drain(relay, relay_recv.at[0]))
+
+    @pl.when(even & ~last_tile)
     def _():
         pl.when(first_tile)(lambda: pl.semaphore_wait(ready.at[0], from_before))
-        for chunk in range(CHUNKS):
-            for g in (me, me + 1):
-                send(relay.at[chunk], late_in.at[chunk, 1], 1, late_recv.at[chunk, 1], (before, g))
+        late_left(relay, (me, me + 1))
 
     load_shift.wait()
     load_blocks.wait()
@@ -223,6 +229,10 @@
 
     pl.when(me > 0)(lambda: drain(rim_in.at[0], rim_recv.at[0]))
     pl.when(me < last)(lambda: drain(rim_in.at[1], rim_recv.at[1]))
+    for side, g in ((0, 0), (1, last)):
+        product = mm_t(gram[:, g * capacity : (g + 1) * capacity], rim_in[side])
+        far_gram[:, side * rim : (side + 1) * rim] = product.astype(jnp.bfloat16)
+
     pl.when(~even & first_tile)(lambda: pl.semaphore_wait(ready.at[0], from_before))
     pl.when((me != last) & ~last_tile)(lambda: pl.semaphore_wait(ready.at[1], from_after))
 
@@ -230,7 +240,7 @@
     def _():
         for chunk in range(CHUNKS):
             drain(late_in.at[chunk, 0], late_recv.at[chunk, 0])
-            send(late_in.at[chunk, 0], late_in.at[chunk, 0], 8, late_recv.at[chunk, 0], (tile, mate))
+            send(late_in.at[chunk, 0], late_in.at[chunk, 0], late_recv.at[chunk, 0], (tile, mate))
 
     for chunk in range(CHUNKS):
         cells = arrived(chunk, slot_in, slot_recv)
@@ -238,26 +248,28 @@
         drain(late_in.at[chunk, 1], late_recv.at[chunk, 1])
         for side, g in ((0, 0), (1, last)):
             cells[g] = (cells[g].astype(jnp.float32) + mm(late_in[chunk, side], rim_in[side])).astype(jnp.bfloat16)
-        adjoint = mm(jnp.concatenate(cells, axis=1), gram[...]).astype(jnp.bfloat16)
+        gathered = jnp.concatenate(cells, axis=1)
+        far = mm(gathered, far_gram[...])
+        far_out[chunk, 1] = far[:, rim:].astype(jnp.bfloat16)
+        send(far_out.at[chunk, 1], far_in.at[chunk, me], part_recv.at[chunk, 0], (after, 0))
+        share[chunk] = far[:, :rim]
+
+        @pl.when(~even)
+        def _():
+            far_out[chunk, 0] = share[chunk].astype(jnp.bfloat16)
+            send(far_out.at[chunk, 0], share_in.at[chunk], share_recv.at[chunk], (tile, mate))
+
+        adjoint = mm(gathered, gram[...]).astype(jnp.bfloat16)
         for g in range(groups):
             cell_out[1, chunk, g] = adjoint[:, g * capacity : (g + 1) * capacity]
         exchange(1, chunk, back_in, back_recv)
-        share_out[chunk] = mm_t(cell_out[1, chunk, (1 - odd) * last], rim_in[1 - odd]).astype(jnp.bfloat16)
-        send(share_out.at[chunk], share_in.at[chunk], 7, share_recv.at[chunk], (tile, mate))
-        share[chunk] = mm_t(cell_out[1, chunk, odd * last], rim_in[odd])
-
-    for chunk in range(CHUNKS):
-        drain(share_in.at[chunk], share_recv.at[chunk])
-        far_out[chunk] = (share[chunk] + share_in[chunk].astype(jnp.float32)).astype(jnp.bfloat16)
-        place = lax.div(me, 2)
-
-        @pl.when(even)
-        def _():
-            send(far_out.at[chunk], far_in.at[chunk, place], 4, part_recv.at[chunk, 1], (before, last))
-
-        @pl.when(~even)
-        def _():
-            send(far_out.at[chunk], far_in.at[chunk, place], 4, part_recv.at[chunk, 0], (after, 0))
+
+    @pl.when(even)
+    def _():
+        for chunk in range(CHUNKS):
+            drain(share_in.at[chunk], share_recv.at[chunk])
+            far_out[chunk, 0] = (share[chunk] + share_in[chunk].astype(jnp.float32)).astype(jnp.bfloat16)
+            send(far_out.at[chunk, 0], far_in.at[chunk, lax.div(me, 2)], part_recv.at[chunk, 1], (before, last))
 
     for chunk in range(CHUNKS):
         part = piece(chunk)
@@ -268,50 +280,56 @@
 
         @pl.when(me < last)
         def _():
-            send(part_out.at[chunk, 0], part_in.at[chunk, 0], 5, part_recv.at[chunk, 0], (tile, up))
+            send(part_out.at[chunk, 0], part_in.at[chunk, 0], part_recv.at[chunk, 0], (tile, up))
 
         @pl.when(me > 0)
         def _():
-            send(part_out.at[chunk, 1], part_in.at[chunk, 1], 5, part_recv.at[chunk, 1], (tile, down))
+            send(part_out.at[chunk, 1], part_in.at[chunk, 1], part_recv.at[chunk, 1], (tile, down))
 
         result[part, :] = mm_t(returned, ip[2 * rim :, :])
 
-    for chunk in range(CHUNKS):
-        part = piece(chunk)
-        for side, where, pick, end in ((0, lead, left_pick, 0), (1, tail, right_pick, last)):
-
-            @pl.when(me != end)
-            def _():
-                drain(part_in.at[chunk, side], part_recv.at[chunk, side])
-                result[part, where] += mm_t(part_in[chunk, side], pick)
-
-            @pl.when(me == end)
-            def _():
-                drain(far_in.at[chunk], part_recv.at[chunk, side])
-                total = result[part, where]
-                for g in range(groups // 2):
-                    total = total + mm_t(far_in[chunk, g], pick)
-                result[part, where] = total
+    borders = [
+        (chunk, piece(chunk), *border)
+        for chunk in range(CHUNKS)
+        for border in ((0, lead, left_pick, 0), (1, tail, right_pick, last))
+    ]
+    for chunk, part, side, where, pick, end in borders:
+
+        @pl.when(me != end)
+        def _():
+            drain(part_in.at[chunk, side], part_recv.at[chunk, side])
+            result[part, where] += mm_t(part_in[chunk, side], pick)
+
+    for chunk, part, side, where, pick, end in borders:
+        shares = middle if side else groups
+
+        @pl.when(me == end)
+        def _():
+            drain(far_in.at[chunk, 0:shares], part_recv.at[chunk, side])
+            total = result[part, where]
+            for g in range(shares):
+                total = total + mm_t(far_in[chunk, g], pick)
+            result[part, where] = total
 
     drain(cell_out.at[:, :, 0:last], send_sem.at[0])
-    drain(far_out, send_sem.at[4])
-    drain(share_out, send_sem.at[7])
-    pl.when(even)(lambda: drain(late_in, send_sem.at[1]))
-    pl.when(~even)(lambda: drain(late_in.at[:, 0], send_sem.at[8]))
-
-    pl.when(me == 0)(lambda: drain(far_in.at[:, 0 : groups // 2 - 1], send_sem.at[6]))
-    pl.when(me == last)(lambda: drain(far_in, send_sem.at[1]))
+    drain(far_out, send_sem.at[0])
+    pl.when(even & ~last_tile)(lambda: drain(late_in, send_sem.at[0]))
+    pl.when((me == 0) & last_tile)(lambda: drain(far_in, send_sem.at[0]))
+    pl.when(~even)(lambda: drain(late_in.at[:, 0], send_sem.at[0]))
+
+    pl.when((me == 0) & ~last_tile)(lambda: drain(far_in.at[:, 0 : groups // 2 - 1], send_sem.at[0]))
+    pl.when(me == last)(lambda: drain(far_in.at[:, 0 : groups // 2], send_sem.at[0]))
 
     @pl.when((me == 0) | (me == last))
     def _():
-        drain(edge_out.at[:, 0], send_sem.at[2])
-        drain(rim_out.at[0:last], send_sem.at[3])
-        drain(part_out.at[:, 0], send_sem.at[5])
+        drain(edge_out.at[:, 0], send_sem.at[0])
+        drain(rim_out.at[0:last], send_sem.at[0])
+        drain(part_out.at[:, 0], send_sem.at[0])
 
     @pl.when((me != 0) & (me != last))
     def _():
-        drain(edge_out, send_sem.at[2])
-        drain(part_out, send_sem.at[5])
+        drain(edge_out, send_sem.at[0])
+        drain(part_out, send_sem.at[0])
 
 
 def in_hbm(array):
@@ -352,11 +370,13 @@
             pltpu.VMEM((2, rim, capacity), half),
             pltpu.VMEM((2, CHUNKS, groups, height, capacity), half),
             cells, cells,
+            pltpu.VMEM((slots, 2 * rim), half),
             pltpu.VMEM((CHUNKS, height, rim), single),
-            strip, strip, strip,
-            pltpu.VMEM((CHUNKS, groups // 2, height, rim), half),
+            strip,
+            sides,
+            pltpu.VMEM((CHUNKS, groups, height, rim), half),
             sides, sides,
-            pltpu.SemaphoreType.REGULAR((2,)), dma((8,)), dma((9,)), dma((CHUNKS, 2)), dma((1,)), dma((CHUNKS, 2)), dma((2,)), dma((CHUNKS,)), dma((CHUNKS,)), dma((CHUNKS,)),
+            pltpu.SemaphoreType.REGULAR((2,)), dma((8,)), dma((1,)), dma((CHUNKS, 2)), dma((1,)), dma((CHUNKS, 2)), dma((2,)), dma((CHUNKS,)), dma((CHUNKS,)), dma((CHUNKS,)),
             dma((CHUNKS, 2)),
         ],
         compiler_params=pltpu.CompilerParams(collective_id=0, has_side_effects=True, vmem_limit_bytes=53 * 2**20),

time: 20 us -> 19.2 us (0.960); the launches traced: 19.9 us -> 18.9 us
  Pallas kernels: 19 us -> 18 us
    pallas_call x1, Pallas kernels: 19 us -> 18 us  [on_device(): pl.pallas_call(functools.partial(kernel, tiles, groups, rim), out_shape=j...]
where the time goes in v3:
time: 19.2 us; the launch traced here: 18.9 us
  Pallas kernels  18 us (94%)
  local copies, waits for them, and re-layouts  0.88 us (5%)
    pallas_call x1, Pallas kernels, on_device(): pl.pallas_call(functools.partial(kernel, tiles, groups, rim), out_shape=j...  18 us
    unnamed x1, local copies, waits for them, and re-layouts  0.88 us

profile of v3, /device:TPU:0, one launch (start us, length us, event | category | flops | bytes accessed | tf_op | source)
XLA Modules:
  0.0 18.9 jit_solution(15222949690231641557)
XLA Ops:
  0.0 18.0 %shard_map.64 = f32[256,768]{1,0:T(8,128)S(1)} custom-call(f32[256,768]{1,0:T(8,128)} %field_hbm.1, bf16[1024,384]{1,0:T(8,128)(2,1)} %interp_hbm.1, bf16[2,3,256,256]{3,2,1,0:T(8,128)(2,1)} %blocks_hbm.1, s32[1,384]{1,0:T(1,128)} %bitcast.1, s32[2,128]{1,0:T(2,128)} %index_hbm.1, s32[2,3]{1,0:T(2,128)} %shift_hbm.1), custom_call_target="tpu_custom_call" | custom-call | tf_op jit(solution)/shard_map/pallas_call | solution.py:352
  18.0 0.9 %copy.8 = f32[256,768]{1,0:T(8,128)} copy(f32[256,768]{1,0:T(8,128)S(1)} %shard_map.64) | data formatting | bytes 1572864

commit v4 on v3

--- a/solution.py
+++ b/solution.py
@@ -9,6 +9,7 @@
 
 MESH = pl.DeviceIdType.MESH
 CHUNKS = 2
+FAR = 2
 
 
 def mm(left, right):
@@ -21,9 +22,9 @@
 
 def kernel(
     tiles, groups, rim, field_hbm, interp_hbm, blocks_hbm, owner_hbm, index_hbm, shift_hbm, result,
-    field, interp, blocks, owner, index, shift, ip, conv, gram, base,
-    edge_out, edge_in, relay, late_in, rim_out, rim_in, cell_out, slot_in, back_in, far_gram, share, share_in, far_out, far_in, part_out, part_in,
-    ready, load_sem, send_sem, edge_recv, relay_recv, late_recv, rim_recv, slot_recv, back_recv, share_recv, part_recv,
+    field, interp, blocks, owner, index, shift, ip, conv, gram, base, returned,
+    edge_out, edge_in, relay, late_in, rim_out, rim_in, cell_out, slot_in, back_in, gathered, far_gram, share, share_in, far_out, far_in, part_out, part_in,
+    ready, load_sem, send_sem, edge_recv, relay_recv, late_recv, rim_recv, slot_recv, back_recv, share_recv, part_recv, far_recv,
 ):
     rows, columns = field.shape
     extended, points = interp.shape
@@ -31,6 +32,7 @@
     slots = owned * size
     capacity = slots // groups
     height = rows // CHUNKS
+    step = CHUNKS // FAR
     last = groups - 1
     tile, me = lax.axis_index("tile"), lax.axis_index("conv")
     after, before = lax.rem(tile + 1, tiles), lax.rem(tile + tiles - 1, tiles)
@@ -131,11 +133,11 @@
 
         @pl.when(me < last)
         def _():
-            send(edge_out.at[chunk, 0], edge_in.at[chunk, 0], edge_recv.at[chunk, 0], (tile, up))
+            send(edge_out.at[chunk, 0], edge_in.at[chunk, 0], edge_recv.at[chunk], (tile, up))
 
         @pl.when(me > 0)
         def _():
-            send(edge_out.at[chunk, 1], edge_in.at[chunk, 1], edge_recv.at[chunk, 1], (tile, down))
+            send(edge_out.at[chunk, 1], edge_in.at[chunk, 1], edge_recv.at[chunk], (tile, down))
 
     @pl.when((me == 0) & ~last_tile)
     def _():
@@ -144,9 +146,10 @@
             send(edge_out.at[:, 1], relay, relay_recv.at[0], (tile, g))
 
     def late_right():
-        for chunk in range(CHUNKS):
+        for part in range(FAR):
             for g in range(1, groups, 2):
-                send(edge_out.at[chunk, 0], late_in.at[chunk, 0], late_recv.at[chunk, 0], (after, g))
+                source = edge_out.at[part * step : (part + 1) * step, 0]
+                send(source, late_in.at[part, 0], late_recv.at[part, 0], (after, g))
 
     pl.when((me == last) & last_tile)(late_right)
 
@@ -183,15 +186,31 @@
     @pl.when(me == last)
     def _():
         for g in range(last):
-            send(rim_out.at[g], rim_in.at[1], rim_recv.at[1], (tile, g))
+            send(rim_out.at[g], rim_in.at[1], rim_recv.at[0], (tile, g))
 
     ip[2 * rim :, :] = mm_t(interp[rim : extended - rim, :], placement).astype(jnp.bfloat16)
     load_inner.wait()
     base[...] = mm(field[...].astype(jnp.bfloat16), ip[2 * rim :, :])
 
-    for chunk in range(CHUNKS):
-        pl.when(me > 0)(lambda: drain(edge_in.at[chunk, 0], edge_recv.at[chunk, 0]))
-        pl.when(me < last)(lambda: drain(edge_in.at[chunk, 1], edge_recv.at[chunk, 1]))
+    load_shift.wait()
+    load_blocks.wait()
+
+    def build_gram():
+        for j in range(owned):
+            for s in range(owned):
+                total = jnp.zeros((size, size), jnp.float32)
+                for c in range(bands):
+                    reads = lax.rem(j + shift[j : j + 1, c : c + 1], owned) == s
+                    total = total + jnp.where(reads, 1.0, 0.0) * blocks[j, c].astype(jnp.float32)
+                conv[s * size : (s + 1) * size, j * size : (j + 1) * size] = total.astype(jnp.bfloat16)
+        gram[...] = mm_t(conv[...], conv[...]).astype(jnp.bfloat16)
+
+    outer = (me == 0) | (me == last)
+    pl.when(~outer)(build_gram)
+
+    for chunk in range(CHUNKS):
+        pl.when(outer)(lambda: drain(edge_in.at[chunk, 0], edge_recv.at[chunk]))
+        pl.when(~outer)(lambda: drain(edge_in.at[chunk], edge_recv.at[chunk]))
         edges = jnp.concatenate([edge_in[chunk, 0], edge_in[chunk, 1]], axis=1)
         subgrid = (base[piece(chunk), :] + mm(edges, ip[0 : 2 * rim, :])).astype(jnp.bfloat16)
         for g in range(groups):
@@ -204,9 +223,10 @@
         late_right()
 
     def late_left(source, cores):
-        for chunk in range(CHUNKS):
+        for part in range(FAR):
             for g in cores:
-                send(source.at[chunk], late_in.at[chunk, 1], late_recv.at[chunk, 1], (before, g))
+                rows_of = source.at[part * step : (part + 1) * step]
+                send(rows_of, late_in.at[part, 1], late_recv.at[part, 1], (before, g))
 
     pl.when(last_tile & (me == 0))(lambda: late_left(edge_out.at[:, 1], range(groups)))
     pl.when(even & (me != 0) & ~last_tile)(lambda: drain(relay, relay_recv.at[0]))
@@ -216,19 +236,10 @@
         pl.when(first_tile)(lambda: pl.semaphore_wait(ready.at[0], from_before))
         late_left(relay, (me, me + 1))
 
-    load_shift.wait()
-    load_blocks.wait()
-    for j in range(owned):
-        for s in range(owned):
-            total = jnp.zeros((size, size), jnp.float32)
-            for c in range(bands):
-                reads = lax.rem(j + shift[j : j + 1, c : c + 1], owned) == s
-                total = total + jnp.where(reads, 1.0, 0.0) * blocks[j, c].astype(jnp.float32)
-            conv[s * size : (s + 1) * size, j * size : (j + 1) * size] = total.astype(jnp.bfloat16)
-    gram[...] = mm_t(conv[...], conv[...]).astype(jnp.bfloat16)
-
-    pl.when(me > 0)(lambda: drain(rim_in.at[0], rim_recv.at[0]))
-    pl.when(me < last)(lambda: drain(rim_in.at[1], rim_recv.at[1]))
+    pl.when(outer)(build_gram)
+
+    pl.when(outer)(lambda: drain(rim_in.at[0], rim_recv.at[0]))
+    pl.when(~outer)(lambda: drain(rim_in, rim_recv.at[0]))
     for side, g in ((0, 0), (1, last)):
         product = mm_t(gram[:, g * capacity : (g + 1) * capacity], rim_in[side])
         far_gram[:, side * rim : (side + 1) * rim] = product.astype(jnp.bfloat16)
@@ -236,80 +247,97 @@
     pl.when(~even & first_tile)(lambda: pl.semaphore_wait(ready.at[0], from_before))
     pl.when((me != last) & ~last_tile)(lambda: pl.semaphore_wait(ready.at[1], from_after))
 
+    def pass_on(part):
+        drain(late_in.at[part, 0], late_recv.at[part, 0])
+        send(late_in.at[part, 0], late_in.at[part, 0], late_recv.at[part, 0], (tile, mate))
+
     @pl.when(~even)
     def _():
-        for chunk in range(CHUNKS):
-            drain(late_in.at[chunk, 0], late_recv.at[chunk, 0])
-            send(late_in.at[chunk, 0], late_in.at[chunk, 0], late_recv.at[chunk, 0], (tile, mate))
-
-    for chunk in range(CHUNKS):
+        for part in range(FAR):
+            pass_on(part)
+
+    for chunk in range(CHUNKS):
+        far_part, row = chunk // step, chunk % step
+        if row == 0:
+            pl.when(even)(lambda: drain(late_in.at[far_part, 0], late_recv.at[far_part, 0]))
+            drain(late_in.at[far_part, 1], late_recv.at[far_part, 1])
+        added = [mm(late_in[far_part, side, row], rim_in[side]) for side in range(2)]
         cells = arrived(chunk, slot_in, slot_recv)
-        pl.when(even)(lambda: drain(late_in.at[chunk, 0], late_recv.at[chunk, 0]))
-        drain(late_in.at[chunk, 1], late_recv.at[chunk, 1])
         for side, g in ((0, 0), (1, last)):
-            cells[g] = (cells[g].astype(jnp.float32) + mm(late_in[chunk, side], rim_in[side])).astype(jnp.bfloat16)
-        gathered = jnp.concatenate(cells, axis=1)
-        far = mm(gathered, far_gram[...])
-        far_out[chunk, 1] = far[:, rim:].astype(jnp.bfloat16)
-        send(far_out.at[chunk, 1], far_in.at[chunk, me], part_recv.at[chunk, 0], (after, 0))
-        share[chunk] = far[:, :rim]
-
-        @pl.when(~even)
-        def _():
-            far_out[chunk, 0] = share[chunk].astype(jnp.bfloat16)
-            send(far_out.at[chunk, 0], share_in.at[chunk], share_recv.at[chunk], (tile, mate))
-
-        adjoint = mm(gathered, gram[...]).astype(jnp.bfloat16)
+            cells[g] = (cells[g].astype(jnp.float32) + added[side]).astype(jnp.bfloat16)
+        gathered[chunk] = jnp.concatenate(cells, axis=1)
+
+        def far_shares():
+            far = mm(gathered[chunk], far_gram[...])
+            far_out[chunk, 1] = far[:, rim:].astype(jnp.bfloat16)
+            send(far_out.at[chunk, 1], far_in.at[chunk, me], far_recv.at[chunk], (after, 0))
+            share[chunk] = far[:, :rim]
+
+            @pl.when(~even)
+            def _():
+                far_out[chunk, 0] = share[chunk].astype(jnp.bfloat16)
+                send(far_out.at[chunk, 0], share_in.at[chunk], share_recv.at[0], (tile, mate))
+
+        pl.when(last_tile)(far_shares)
+        adjoint = mm(gathered[chunk], gram[...]).astype(jnp.bfloat16)
         for g in range(groups):
             cell_out[1, chunk, g] = adjoint[:, g * capacity : (g + 1) * capacity]
         exchange(1, chunk, back_in, back_recv)
+        pl.when(~last_tile)(far_shares)
 
     @pl.when(even)
     def _():
-        for chunk in range(CHUNKS):
-            drain(share_in.at[chunk], share_recv.at[chunk])
-            far_out[chunk, 0] = (share[chunk] + share_in[chunk].astype(jnp.float32)).astype(jnp.bfloat16)
-            send(far_out.at[chunk, 0], far_in.at[chunk, lax.div(me, 2)], part_recv.at[chunk, 1], (before, last))
-
-    for chunk in range(CHUNKS):
-        part = piece(chunk)
-        returned = jnp.concatenate(arrived(chunk, back_in, back_recv), axis=1)
-        rims = mm_t(returned, ip[0 : 2 * rim, :]).astype(jnp.bfloat16)
+        drain(share_in, share_recv.at[0])
+        far_out[:, 0] = (share[...] + share_in[...].astype(jnp.float32)).astype(jnp.bfloat16)
+        send(far_out.at[:, 0], far_in.at[:, lax.div(me, 2)], far_recv.at[0], (before, last))
+
+    for chunk in range(CHUNKS):
+        back = jnp.concatenate(arrived(chunk, back_in, back_recv), axis=1)
+        returned[chunk * height : (chunk + 1) * height, :] = back
+        rims = mm_t(back, ip[0 : 2 * rim, :]).astype(jnp.bfloat16)
         part_out[chunk, 0] = rims[:, rim:]
         part_out[chunk, 1] = rims[:, :rim]
 
         @pl.when(me < last)
         def _():
-            send(part_out.at[chunk, 0], part_in.at[chunk, 0], part_recv.at[chunk, 0], (tile, up))
+            send(part_out.at[chunk, 0], part_in.at[chunk, 0], part_recv.at[chunk], (tile, up))
 
         @pl.when(me > 0)
         def _():
-            send(part_out.at[chunk, 1], part_in.at[chunk, 1], part_recv.at[chunk, 1], (tile, down))
-
-        result[part, :] = mm_t(returned, ip[2 * rim :, :])
-
-    borders = [
-        (chunk, piece(chunk), *border)
-        for chunk in range(CHUNKS)
-        for border in ((0, lead, left_pick, 0), (1, tail, right_pick, last))
-    ]
-    for chunk, part, side, where, pick, end in borders:
-
-        @pl.when(me != end)
-        def _():
-            drain(part_in.at[chunk, side], part_recv.at[chunk, side])
-            result[part, where] += mm_t(part_in[chunk, side], pick)
-
-    for chunk, part, side, where, pick, end in borders:
-        shares = middle if side else groups
-
-        @pl.when(me == end)
-        def _():
-            drain(far_in.at[chunk, 0:shares], part_recv.at[chunk, side])
-            total = result[part, where]
-            for g in range(shares):
-                total = total + mm_t(far_in[chunk, g], pick)
-            result[part, where] = total
+            send(part_out.at[chunk, 1], part_in.at[chunk, 1], part_recv.at[chunk], (tile, down))
+
+        if chunk % step == step - 1:
+            part = slice((chunk + 1 - step) * height, (chunk + 1) * height)
+            result[part, :] = mm_t(returned[part, :], ip[2 * rim :, :])
+
+    for chunk in range(CHUNKS):
+        part = piece(chunk)
+        pl.when(outer)(lambda: drain(part_in.at[chunk, 0], part_recv.at[chunk]))
+        pl.when(~outer)(lambda: drain(part_in.at[chunk], part_recv.at[chunk]))
+
+        @pl.when(me > 0)
+        def _():
+            result[part, lead] += mm_t(part_in[chunk, 0], left_pick)
+
+        @pl.when(me < last)
+        def _():
+            result[part, tail] += mm_t(part_in[chunk, 1], right_pick)
+
+    def add_shares(chunk, where, pick, shares):
+        arrived_shares = jnp.concatenate([far_in[chunk, g] for g in range(shares)], axis=1)
+        result[piece(chunk), where] += mm_t(arrived_shares, jnp.concatenate([pick] * shares, axis=1))
+
+    @pl.when(me == 0)
+    def _():
+        for chunk in range(CHUNKS):
+            drain(far_in.at[chunk], far_recv.at[chunk])
+            add_shares(chunk, lead, left_pick, groups)
+
+    @pl.when(me == last)
+    def _():
+        drain(far_in.at[:, 0:middle], far_recv.at[0])
+        for chunk in range(CHUNKS):
+            add_shares(chunk, tail, right_pick, middle)
 
     drain(cell_out.at[:, :, 0:last], send_sem.at[0])
     drain(far_out, send_sem.at[0])
@@ -365,19 +393,21 @@
             pltpu.VMEM((slots, slots), half),
             pltpu.VMEM((slots, slots), half),
             pltpu.VMEM((rows, slots), single),
-            sides, sides, strip, sides,
+            pltpu.VMEM((rows, slots), half),
+            sides, sides, strip, pltpu.VMEM((FAR, 2, CHUNKS // FAR, height, rim), half),
             pltpu.VMEM((groups, rim, capacity), half),
             pltpu.VMEM((2, rim, capacity), half),
             pltpu.VMEM((2, CHUNKS, groups, height, capacity), half),
             cells, cells,
+            pltpu.VMEM((CHUNKS, height, slots), half),
             pltpu.VMEM((slots, 2 * rim), half),
             pltpu.VMEM((CHUNKS, height, rim), single),
             strip,
             sides,
             pltpu.VMEM((CHUNKS, groups, height, rim), half),
             sides, sides,
-            pltpu.SemaphoreType.REGULAR((2,)), dma((8,)), dma((1,)), dma((CHUNKS, 2)), dma((1,)), dma((CHUNKS, 2)), dma((2,)), dma((CHUNKS,)), dma((CHUNKS,)), dma((CHUNKS,)),
-            dma((CHUNKS, 2)),
+            pltpu.SemaphoreType.REGULAR((2,)), dma((8,)), dma((1,)), dma((CHUNKS,)), dma((1,)), dma((FAR, 2)),
+            dma((1,)), dma((CHUNKS,)), dma((CHUNKS,)), dma((1,)), dma((CHUNKS,)), dma((CHUNKS,)),
         ],
         compiler_params=pltpu.CompilerParams(collective_id=0, has_side_effects=True, vmem_limit_bytes=53 * 2**20),
     )(field, interp, conv_blocks, *[in_hbm(small) for small in (owner.reshape(1, -1), edge_index, band_shift)])

time: 19.2 us -> 18.9 us (0.984); the launches traced: 18.9 us -> 18.8 us
  no operation moved by 1% of the time
where the time goes in v4:
time: 18.9 us; the launch traced here: 18.8 us
  Pallas kernels  17.9 us (95%)
  local copies, waits for them, and re-layouts  0.88 us (5%)
    pallas_call x1, Pallas kernels, on_device(): pl.pallas_call(functools.partial(kernel, tiles, groups, rim), out_shape=j...  17.9 us
    unnamed x1, local copies, waits for them, and re-layouts  0.88 us

profile of v4, /device:TPU:0, one launch (start us, length us, event | category | flops | bytes accessed | tf_op | source)
XLA Modules:
  0.0 18.8 jit_solution(5623615785329449792)
XLA Ops:
  0.0 17.9 %shard_map.64 = f32[256,768]{1,0:T(8,128)S(1)} custom-call(f32[256,768]{1,0:T(8,128)} %field_hbm.1, bf16[1024,384]{1,0:T(8,128)(2,1)} %interp_hbm.1, bf16[2,3,256,256]{3,2,1,0:T(8,128)(2,1)} %blocks_hbm.1, s32[1,384]{1,0:T(1,128)} %bitcast.1, s32[2,128]{1,0:T(2,128)} %index_hbm.1, s32[2,3]{1,0:T(2,128)} %shift_hbm.1), custom_call_target="tpu_custom_call" | custom-call | tf_op jit(solution)/shard_map/pallas_call | solution.py:380
  17.9 0.9 %copy.8 = f32[256,768]{1,0:T(8,128)} copy(f32[256,768]{1,0:T(8,128)S(1)} %shard_map.64) | data formatting | bytes 1572864

commit v5 on v4

--- a/solution.py
+++ b/solution.py
@@ -47,9 +47,12 @@
     odd = lax.rem(me, 2)
     even = odd == 0
     mate = me + 1 - 2 * odd
+    pre_last = (tile == tiles - 2) & ~first_tile
+    hands_right = pre_last & ~even & (me != last)
+    hands_on = (first_tile & ~even) | (~first_tile & ~last_tile & even)
 
     def meet(lower, upper):
-        return (upper == 0) | (lower == last) | (upper == lower - lax.rem(lower, 2))
+        return (upper == 0) | (lower == last) | (lax.div(lower, 2) == lax.div(upper, 2))
 
     with_before = [meet(g, me) for g in range(groups)]
     with_after = [meet(me, g) for g in range(groups)]
@@ -139,17 +142,31 @@
         def _():
             send(edge_out.at[chunk, 1], edge_in.at[chunk, 1], edge_recv.at[chunk], (tile, down))
 
-    @pl.when((me == 0) & ~last_tile)
+    def hand_round(cores):
+        for g in cores:
+            send(edge_out.at[:, 1], relay, relay_recv.at[0], (tile, g))
+
+    pl.when((me == 0) & first_tile)(lambda: hand_round(range(1, groups, 2)))
+
+    @pl.when((me == 0) & ~first_tile & ~last_tile)
     def _():
         relay[...] = edge_out[:, 1]
-        for g in range(2, groups, 2):
-            send(edge_out.at[:, 1], relay, relay_recv.at[0], (tile, g))
+        hand_round(range(2, groups, 2))
+
+    def send_right(source, cores):
+        for part in range(FAR):
+            for g in cores:
+                rows_of = source.at[part * step : (part + 1) * step]
+                send(rows_of, late_in.at[part, 0], late_recv.at[part, 0], (after, g))
 
     def late_right():
-        for part in range(FAR):
-            for g in range(1, groups, 2):
-                source = edge_out.at[part * step : (part + 1) * step, 0]
-                send(source, late_in.at[part, 0], late_recv.at[part, 0], (after, g))
+        pl.when(pre_last)(lambda: send_right(edge_out.at[:, 0], [last]))
+        pl.when(~pre_last)(lambda: send_right(edge_out.at[:, 0], range(1, groups, 2)))
+
+    @pl.when((me == last) & pre_last)
+    def _():
+        for g in range(1, last, 2):
+            send(edge_out.at[:, 0], relay, relay_recv.at[0], (tile, g))
 
     pl.when((me == last) & last_tile)(late_right)
 
@@ -208,6 +225,12 @@
     outer = (me == 0) | (me == last)
     pl.when(~outer)(build_gram)
 
+    @pl.when(hands_right)
+    def _():
+        drain(relay, relay_recv.at[0])
+        pl.semaphore_wait(ready.at[1], from_after)
+        send_right(relay, [me])
+
     for chunk in range(CHUNKS):
         pl.when(outer)(lambda: drain(edge_in.at[chunk, 0], edge_recv.at[chunk]))
         pl.when(~outer)(lambda: drain(edge_in.at[chunk], edge_recv.at[chunk]))
@@ -228,13 +251,13 @@
                 rows_of = source.at[part * step : (part + 1) * step]
                 send(rows_of, late_in.at[part, 1], late_recv.at[part, 1], (before, g))
 
-    pl.when(last_tile & (me == 0))(lambda: late_left(edge_out.at[:, 1], range(groups)))
-    pl.when(even & (me != 0) & ~last_tile)(lambda: drain(relay, relay_recv.at[0]))
-
-    @pl.when(even & ~last_tile)
-    def _():
+    pl.when(last_tile & (me == 0))(lambda: late_left(edge_out.at[:, 1], range(0, groups, 2)))
+
+    @pl.when(hands_on)
+    def _():
+        pl.when(me != 0)(lambda: drain(relay, relay_recv.at[0]))
         pl.when(first_tile)(lambda: pl.semaphore_wait(ready.at[0], from_before))
-        late_left(relay, (me, me + 1))
+        late_left(relay, (me - odd, me - odd + 1))
 
     pl.when(outer)(build_gram)
 
@@ -244,39 +267,50 @@
         product = mm_t(gram[:, g * capacity : (g + 1) * capacity], rim_in[side])
         far_gram[:, side * rim : (side + 1) * rim] = product.astype(jnp.bfloat16)
 
-    pl.when(~even & first_tile)(lambda: pl.semaphore_wait(ready.at[0], from_before))
-    pl.when((me != last) & ~last_tile)(lambda: pl.semaphore_wait(ready.at[1], from_after))
-
-    def pass_on(part):
-        drain(late_in.at[part, 0], late_recv.at[part, 0])
-        send(late_in.at[part, 0], late_in.at[part, 0], late_recv.at[part, 0], (tile, mate))
-
-    @pl.when(~even)
-    def _():
+    pl.when(even & first_tile)(lambda: pl.semaphore_wait(ready.at[0], from_before))
+    pl.when((me != last) & ~last_tile & ~hands_right)(lambda: pl.semaphore_wait(ready.at[1], from_after))
+
+    def pass_on(side):
         for part in range(FAR):
-            pass_on(part)
+            arrival = late_recv.at[part, side]
+            drain(late_in.at[part, side], arrival)
+            send(late_in.at[part, side], late_in.at[part, side], arrival, (tile, mate))
+
+    pl.when(~even)(lambda: pass_on(0))
+    pl.when(even & pre_last)(lambda: pass_on(1))
 
     for chunk in range(CHUNKS):
         far_part, row = chunk // step, chunk % step
         if row == 0:
             pl.when(even)(lambda: drain(late_in.at[far_part, 0], late_recv.at[far_part, 0]))
-            drain(late_in.at[far_part, 1], late_recv.at[far_part, 1])
+            pl.when(~even | ~pre_last)(lambda: drain(late_in.at[far_part, 1], late_recv.at[far_part, 1]))
         added = [mm(late_in[far_part, side, row], rim_in[side]) for side in range(2)]
         cells = arrived(chunk, slot_in, slot_recv)
         for side, g in ((0, 0), (1, last)):
             cells[g] = (cells[g].astype(jnp.float32) + added[side]).astype(jnp.bfloat16)
         gathered[chunk] = jnp.concatenate(cells, axis=1)
 
+        def give(side):
+            send(far_out.at[chunk, side], share_in.at[chunk], share_recv.at[0], (tile, mate))
+
         def far_shares():
             far = mm(gathered[chunk], far_gram[...])
             far_out[chunk, 1] = far[:, rim:].astype(jnp.bfloat16)
-            send(far_out.at[chunk, 1], far_in.at[chunk, me], far_recv.at[chunk], (after, 0))
-            share[chunk] = far[:, :rim]
+
+            @pl.when(last_tile)
+            def _():
+                send(far_out.at[chunk, 1], far_in.at[chunk, me], far_recv.at[chunk], (after, 0))
+
+            @pl.when(even)
+            def _():
+                share[chunk] = far[:, :rim]
+                pl.when(~last_tile)(lambda: give(1))
 
             @pl.when(~even)
             def _():
-                far_out[chunk, 0] = share[chunk].astype(jnp.bfloat16)
-                send(far_out.at[chunk, 0], share_in.at[chunk], share_recv.at[0], (tile, mate))
+                share[chunk] = far[:, rim:]
+                far_out[chunk, 0] = far[:, :rim].astype(jnp.bfloat16)
+                give(0)
 
         pl.when(last_tile)(far_shares)
         adjoint = mm(gathered[chunk], gram[...]).astype(jnp.bfloat16)
@@ -285,11 +319,13 @@
         exchange(1, chunk, back_in, back_recv)
         pl.when(~last_tile)(far_shares)
 
-    @pl.when(even)
-    def _():
+    def add_given(side, place):
         drain(share_in, share_recv.at[0])
-        far_out[:, 0] = (share[...] + share_in[...].astype(jnp.float32)).astype(jnp.bfloat16)
-        send(far_out.at[:, 0], far_in.at[:, lax.div(me, 2)], far_recv.at[0], (before, last))
+        far_out[:, side] = (share[...] + share_in[...].astype(jnp.float32)).astype(jnp.bfloat16)
+        send(far_out.at[:, side], far_in.at[:, lax.div(me, 2)], far_recv.at[0], place)
+
+    pl.when(even)(lambda: add_given(0, (before, last)))
+    pl.when(~even & ~last_tile)(lambda: add_given(1, (after, 0)))
 
     for chunk in range(CHUNKS):
         back = jnp.concatenate(arrived(chunk, back_in, back_recv), axis=1)
@@ -327,25 +363,30 @@
         arrived_shares = jnp.concatenate([far_in[chunk, g] for g in range(shares)], axis=1)
         result[piece(chunk), where] += mm_t(arrived_shares, jnp.concatenate([pick] * shares, axis=1))
 
-    @pl.when(me == 0)
+    def add_by_chip(where, pick):
+        drain(far_in.at[:, 0:middle], far_recv.at[0])
+        for chunk in range(CHUNKS):
+            add_shares(chunk, where, pick, middle)
+
+    @pl.when((me == 0) & first_tile)
     def _():
         for chunk in range(CHUNKS):
             drain(far_in.at[chunk], far_recv.at[chunk])
             add_shares(chunk, lead, left_pick, groups)
 
-    @pl.when(me == last)
-    def _():
-        drain(far_in.at[:, 0:middle], far_recv.at[0])
-        for chunk in range(CHUNKS):
-            add_shares(chunk, tail, right_pick, middle)
+    pl.when((me == 0) & ~first_tile)(lambda: add_by_chip(lead, left_pick))
+    pl.when(me == last)(lambda: add_by_chip(tail, right_pick))
 
     drain(cell_out.at[:, :, 0:last], send_sem.at[0])
     drain(far_out, send_sem.at[0])
-    pl.when(even & ~last_tile)(lambda: drain(late_in, send_sem.at[0]))
-    pl.when((me == 0) & last_tile)(lambda: drain(far_in, send_sem.at[0]))
+    pl.when(hands_on)(lambda: drain(late_in, send_sem.at[0]))
+    pl.when(hands_right)(lambda: drain(relay, send_sem.at[0]))
+    pl.when((me == 0) & last_tile)(lambda: drain(far_in.at[:, 0:middle], send_sem.at[0]))
+    pl.when(even & pre_last)(lambda: drain(late_in.at[:, 1], send_sem.at[0]))
     pl.when(~even)(lambda: drain(late_in.at[:, 0], send_sem.at[0]))
 
-    pl.when((me == 0) & ~last_tile)(lambda: drain(far_in.at[:, 0 : groups // 2 - 1], send_sem.at[0]))
+    pl.when((me == 0) & first_tile)(lambda: drain(far_in.at[:, 0:middle], send_sem.at[0]))
+    pl.when((me == 0) & ~first_tile & ~last_tile)(lambda: drain(far_in.at[:, 0 : middle - 1], send_sem.at[0]))
     pl.when(me == last)(lambda: drain(far_in.at[:, 0 : groups // 2], send_sem.at[0]))
 
     @pl.when((me == 0) | (me == last))

time: 18.9 us -> 18.8 us (level)
  Pallas kernels: 17.9 us -> 17.7 us
where the time goes in v5:
time: 18.8 us; the launch traced here: 18.6 us
  Pallas kernels  17.7 us (94%)
  local copies, waits for them, and re-layouts  0.88 us (5%)
    pallas_call x1, Pallas kernels, on_device(): pl.pallas_call(functools.partial(kernel, tiles, groups, rim), out_shape=j...  17.7 us
    unnamed x1, local copies, waits for them, and re-layouts  0.88 us

profile of v5, /device:TPU:0, one launch (start us, length us, event | category | flops | bytes accessed | tf_op | source)
XLA Modules:
  0.0 18.6 jit_solution(10124523564060412557)
XLA Ops:
  0.0 17.7 %shard_map.64 = f32[256,768]{1,0:T(8,128)S(1)} custom-call(f32[256,768]{1,0:T(8,128)} %field_hbm.1, bf16[1024,384]{1,0:T(8,128)(2,1)} %interp_hbm.1, bf16[2,3,256,256]{3,2,1,0:T(8,128)(2,1)} %blocks_hbm.1, s32[1,384]{1,0:T(1,128)} %bitcast.1, s32[2,128]{1,0:T(2,128)} %index_hbm.1, s32[2,3]{1,0:T(2,128)} %shift_hbm.1), custom_call_target="tpu_custom_call" | custom-call | tf_op jit(solution)/shard_map/pallas_call | solution.py:421
  17.7 0.9 %copy.8 = f32[256,768]{1,0:T(8,128)} copy(f32[256,768]{1,0:T(8,128)S(1)} %shard_map.64) | data formatting | bytes 1572864

commit v6 on v5

--- a/solution.py
+++ b/solution.py
@@ -88,13 +88,13 @@
     inner = slice(rim, columns - rim)
     lead, tail = slice(0, rim), slice(columns - rim, columns)
     load_index = load(index_hbm, index, 0)
-    load_lead = load(field_hbm.at[:, lead], field.at[:, lead], 1)
-    load_tail = load(field_hbm.at[:, tail], field.at[:, tail], 2)
-    load_owner = load(owner_hbm, owner, 3)
-    load_interp = load(interp_hbm, interp, 4)
-    load_inner = load(field_hbm.at[:, inner], field.at[:, inner], 5)
-    load_shift = load(shift_hbm, shift, 6)
-    load_blocks = load(blocks_hbm, blocks, 7)
+    load_lead = load(field_hbm.at[:, lead], field.at[:, lead], 0)
+    load_tail = load(field_hbm.at[:, tail], field.at[:, tail], 0)
+    load_owner = load(owner_hbm, owner, 1)
+    load_interp = load(interp_hbm, interp, 1)
+    load_inner = load(field_hbm.at[:, inner], field.at[:, inner], 2)
+    load_shift = load(shift_hbm, shift, 3)
+    load_blocks = load(blocks_hbm, blocks, 3)
 
     def piece(chunk):
         return slice(chunk * height, (chunk + 1) * height)
@@ -121,12 +121,12 @@
     pl.when(last_tile)(lambda: tell_after(ready.at[0]))
 
     load_index.wait()
+    load_lead.wait()
+    load_tail.wait()
     left_list, right_list = index[0:1, :], index[1:2, :]
     lines = lax.broadcasted_iota(jnp.int32, (rim, rim), 0)
     left_pick = (lines == left_list).astype(jnp.float32).astype(jnp.bfloat16)
     right_pick = (lines + (columns - rim) == right_list).astype(jnp.float32).astype(jnp.bfloat16)
-    load_lead.wait()
-    load_tail.wait()
     for chunk in range(CHUNKS):
         part = piece(chunk)
         edge_out[chunk, 0] = mm(field[part, tail].astype(jnp.bfloat16), right_pick).astype(jnp.bfloat16)
@@ -171,6 +171,7 @@
     pl.when((me == last) & last_tile)(late_right)
 
     load_owner.wait()
+    load_interp.wait()
     owners = owner[...]
     choose = (owners == lax.broadcasted_iota(jnp.int32, (-(-groups // 8) * 8, points), 0)).astype(jnp.float32)
     order = lax.broadcasted_iota(jnp.int32, (points, points), 0) < lax.broadcasted_iota(
@@ -181,7 +182,6 @@
     slot = owners * capacity + rank.astype(jnp.int32)
     placement = (slot == lax.broadcasted_iota(jnp.int32, (slots, points), 0)).astype(jnp.float32)
     placement = placement.astype(jnp.bfloat16)
-    load_interp.wait()
     ip[0:rim, :] = mm_t(interp[0:rim, :], placement).astype(jnp.bfloat16)
     ip[rim : 2 * rim, :] = mm_t(interp[extended - rim :, :], placement).astype(jnp.bfloat16)
 
@@ -336,28 +336,25 @@
 
         @pl.when(me < last)
         def _():
-            send(part_out.at[chunk, 0], part_in.at[chunk, 0], part_recv.at[chunk], (tile, up))
+            send(part_out.at[chunk, 0], part_in.at[chunk, 0], part_recv.at[chunk, 0], (tile, up))
 
         @pl.when(me > 0)
         def _():
-            send(part_out.at[chunk, 1], part_in.at[chunk, 1], part_recv.at[chunk], (tile, down))
+            send(part_out.at[chunk, 1], part_in.at[chunk, 1], part_recv.at[chunk, 1], (tile, down))
 
         if chunk % step == step - 1:
             part = slice((chunk + 1 - step) * height, (chunk + 1) * height)
             result[part, :] = mm_t(returned[part, :], ip[2 * rim :, :])
 
-    for chunk in range(CHUNKS):
-        part = piece(chunk)
-        pl.when(outer)(lambda: drain(part_in.at[chunk, 0], part_recv.at[chunk]))
-        pl.when(~outer)(lambda: drain(part_in.at[chunk], part_recv.at[chunk]))
-
-        @pl.when(me > 0)
-        def _():
-            result[part, lead] += mm_t(part_in[chunk, 0], left_pick)
-
-        @pl.when(me < last)
-        def _():
-            result[part, tail] += mm_t(part_in[chunk, 1], right_pick)
+    def add_rims(side, where, pick):
+        for chunk in range(CHUNKS):
+            drain(part_in.at[chunk, side], part_recv.at[chunk, side])
+            result[piece(chunk), where] += mm_t(part_in[chunk, side], pick)
+
+    pl.when(even)(lambda: add_rims(1, tail, right_pick))
+    pl.when(~even)(lambda: add_rims(0, lead, left_pick))
+    pl.when(even & (me != 0))(lambda: add_rims(0, lead, left_pick))
+    pl.when(~even & (me != last))(lambda: add_rims(1, tail, right_pick))
 
     def add_shares(chunk, where, pick, shares):
         arrived_shares = jnp.concatenate([far_in[chunk, g] for g in range(shares)], axis=1)
@@ -447,8 +444,8 @@
             sides,
             pltpu.VMEM((CHUNKS, groups, height, rim), half),
             sides, sides,
-            pltpu.SemaphoreType.REGULAR((2,)), dma((8,)), dma((1,)), dma((CHUNKS,)), dma((1,)), dma((FAR, 2)),
-            dma((1,)), dma((CHUNKS,)), dma((CHUNKS,)), dma((1,)), dma((CHUNKS,)), dma((CHUNKS,)),
+            pltpu.SemaphoreType.REGULAR((2,)), dma((4,)), dma((1,)), dma((CHUNKS,)), dma((1,)), dma((FAR, 2)),
+            dma((1,)), dma((CHUNKS,)), dma((CHUNKS,)), dma((1,)), dma((CHUNKS, 2)), dma((CHUNKS,)),
         ],
         compiler_params=pltpu.CompilerParams(collective_id=0, has_side_effects=True, vmem_limit_bytes=53 * 2**20),
     )(field, interp, conv_blocks, *[in_hbm(small) for small in (owner.reshape(1, -1), edge_index, band_shift)])

time: 18.8 us -> 18.7 us (level)
  no operation moved by 1% of the time
where the time goes in v6:
time: 18.7 us; the launch traced here: 18.5 us
  Pallas kernels  17.6 us (94%)
  local copies, waits for them, and re-layouts  0.88 us (5%)
    pallas_call x1, Pallas kernels, on_device(): pl.pallas_call(functools.partial(kernel, tiles, groups, rim), out_shape=j...  17.6 us
    unnamed x1, local copies, waits for them, and re-layouts  0.88 us

profile of v6, /device:TPU:0, one launch (start us, length us, event | category | flops | bytes accessed | tf_op | source)
XLA Modules:
  0.0 18.5 jit_solution(14071179704075561360)
XLA Ops:
  0.0 17.6 %shard_map.64 = f32[256,768]{1,0:T(8,128)S(1)} custom-call(f32[256,768]{1,0:T(8,128)} %field_hbm.1, bf16[1024,384]{1,0:T(8,128)(2,1)} %interp_hbm.1, bf16[2,3,256,256]{3,2,1,0:T(8,128)(2,1)} %blocks_hbm.1, s32[1,384]{1,0:T(1,128)} %bitcast.1, s32[2,128]{1,0:T(2,128)} %index_hbm.1, s32[2,3]{1,0:T(2,128)} %shift_hbm.1), custom_call_target="tpu_custom_call" | custom-call | tf_op jit(solution)/shard_map/pallas_call | solution.py:418
  17.6 0.9 %copy.8 = f32[256,768]{1,0:T(8,128)} copy(f32[256,768]{1,0:T(8,128)S(1)} %shard_map.64) | data formatting | bytes 1572864

commit v7 on v6

--- a/solution.py
+++ b/solution.py
@@ -293,31 +293,43 @@
         def give(side):
             send(far_out.at[chunk, side], share_in.at[chunk], share_recv.at[0], (tile, mate))
 
-        def far_shares():
-            far = mm(gathered[chunk], far_gram[...])
-            far_out[chunk, 1] = far[:, rim:].astype(jnp.bfloat16)
-
-            @pl.when(last_tile)
-            def _():
-                send(far_out.at[chunk, 1], far_in.at[chunk, me], far_recv.at[chunk], (after, 0))
-
-            @pl.when(even)
-            def _():
-                share[chunk] = far[:, :rim]
-                pl.when(~last_tile)(lambda: give(1))
-
-            @pl.when(~even)
-            def _():
-                share[chunk] = far[:, rim:]
-                far_out[chunk, 0] = far[:, :rim].astype(jnp.bfloat16)
-                give(0)
-
-        pl.when(last_tile)(far_shares)
+        def last_share():
+            product = mm(gathered[chunk], far_gram[:, rim:])
+            far_out[chunk, 1] = product.astype(jnp.bfloat16)
+            return product
+
+        def first_share():
+            return mm(gathered[chunk], far_gram[:, :rim])
+
+        def give_first(kept):
+            far_out[chunk, 0] = kept.astype(jnp.bfloat16)
+            give(0)
+
+        @pl.when(last_tile)
+        def _():
+            last_share()
+            send(far_out.at[chunk, 1], far_in.at[chunk, me], far_recv.at[chunk], (after, 0))
+
         adjoint = mm(gathered[chunk], gram[...]).astype(jnp.bfloat16)
         for g in range(groups):
             cell_out[1, chunk, g] = adjoint[:, g * capacity : (g + 1) * capacity]
         exchange(1, chunk, back_in, back_recv)
-        pl.when(~last_tile)(far_shares)
+
+        @pl.when(even)
+        def _():
+            share[chunk] = first_share()
+
+        pl.when(~even)(lambda: give_first(first_share()))
+
+        @pl.when(~last_tile)
+        def _():
+            kept = last_share()
+
+            @pl.when(~even)
+            def _():
+                share[chunk] = kept
+
+            pl.when(even)(lambda: give(1))
 
     def add_given(side, place):
         drain(share_in, share_recv.at[0])

time: 18.7 us -> 18.7 us (level)
  no operation moved by 1% of the time
where the time goes in v7:
time: 18.7 us; the launch traced here: 18.5 us
  Pallas kernels  17.6 us (94%)
  local copies, waits for them, and re-layouts  0.88 us (5%)
    pallas_call x1, Pallas kernels, on_device(): pl.pallas_call(functools.partial(kernel, tiles, groups, rim), out_shape=j...  17.6 us
    unnamed x1, local copies, waits for them, and re-layouts  0.88 us

profile of v7, /device:TPU:0, one launch (start us, length us, event | category | flops | bytes accessed | tf_op | source)
XLA Modules:
  0.0 18.5 jit_solution(10911016442948696800)
XLA Ops:
  0.0 17.6 %shard_map.64 = f32[256,768]{1,0:T(8,128)S(1)} custom-call(f32[256,768]{1,0:T(8,128)} %field_hbm.1, bf16[1024,384]{1,0:T(8,128)(2,1)} %interp_hbm.1, bf16[2,3,256,256]{3,2,1,0:T(8,128)(2,1)} %blocks_hbm.1, s32[1,384]{1,0:T(1,128)} %bitcast.1, s32[2,128]{1,0:T(2,128)} %index_hbm.1, s32[2,3]{1,0:T(2,128)} %shift_hbm.1), custom_call_target="tpu_custom_call" | custom-call | tf_op jit(solution)/shard_map/pallas_call | solution.py:430
  17.6 0.9 %copy.8 = f32[256,768]{1,0:T(8,128)} copy(f32[256,768]{1,0:T(8,128)S(1)} %shard_map.64) | data formatting | bytes 1572864

commit v8 on v7

--- a/solution.py
+++ b/solution.py
@@ -72,24 +72,25 @@
     def tell_after(semaphore):
         tell(semaphore, after, with_after)
 
+    def load(source, target, at):
+        copy = pltpu.make_async_copy(source, target, load_sem.at[at])
+        copy.start()
+        return copy
+
+    def drain(ref, semaphore):
+        pltpu.make_async_copy(ref, ref, semaphore).wait()
+
+    inner = slice(rim, columns - rim)
+    lead, tail = slice(0, rim), slice(columns - rim, columns)
+    load_lead = load(field_hbm.at[:, lead], field.at[:, lead], 0)
+    load_tail = load(field_hbm.at[:, tail], field.at[:, tail], 0)
+    load_index = load(index_hbm, index, 0)
+
     pl.when(first_tile)(lambda: tell_before(barrier))
     pl.when(~last_tile)(lambda: tell_after(barrier))
     for peer in peers:
         signal(barrier, (tile, peer))
 
-    def load(source, target, at):
-        copy = pltpu.make_async_copy(source, target, load_sem.at[at])
-        copy.start()
-        return copy
-
-    def drain(ref, semaphore):
-        pltpu.make_async_copy(ref, ref, semaphore).wait()
-
-    inner = slice(rim, columns - rim)
-    lead, tail = slice(0, rim), slice(columns - rim, columns)
-    load_index = load(index_hbm, index, 0)
-    load_lead = load(field_hbm.at[:, lead], field.at[:, lead], 0)
-    load_tail = load(field_hbm.at[:, tail], field.at[:, tail], 0)
     load_owner = load(owner_hbm, owner, 1)
     load_interp = load(interp_hbm, interp, 1)
     load_inner = load(field_hbm.at[:, inner], field.at[:, inner], 2)

time: 18.7 us -> 18.7 us (level)
  no operation moved by 1% of the time
where the time goes in v8:
time: 18.7 us; the launch traced here: 18.5 us
  Pallas kernels  17.6 us (94%)
  local copies, waits for them, and re-layouts  0.88 us (5%)
    pallas_call x1, Pallas kernels, on_device(): pl.pallas_call(functools.partial(kernel, tiles, groups, rim), out_shape=j...  17.6 us
    unnamed x1, local copies, waits for them, and re-layouts  0.88 us

profile of v8, /device:TPU:0, one launch (start us, length us, event | category | flops | bytes accessed | tf_op | source)
XLA Modules:
  0.0 18.5 jit_solution(4580262886892412474)
XLA Ops:
  0.0 17.6 %shard_map.64 = f32[256,768]{1,0:T(8,128)S(1)} custom-call(f32[256,768]{1,0:T(8,128)} %field_hbm.1, bf16[1024,384]{1,0:T(8,128)(2,1)} %interp_hbm.1, bf16[2,3,256,256]{3,2,1,0:T(8,128)(2,1)} %blocks_hbm.1, s32[1,384]{1,0:T(1,128)} %bitcast.1, s32[2,128]{1,0:T(2,128)} %index_hbm.1, s32[2,3]{1,0:T(2,128)} %shift_hbm.1), custom_call_target="tpu_custom_call" | custom-call | tf_op jit(solution)/shard_map/pallas_call | solution.py:431
  17.6 0.9 %copy.8 = f32[256,768]{1,0:T(8,128)} copy(f32[256,768]{1,0:T(8,128)S(1)} %shard_map.64) | data formatting | bytes 1572864
